TPU v7x, 128 devices: a whole 4x4x4 slice. The times are simulated.
128 devices in a mesh: rows: 4 (over x_lo, core), cols: 4 (over y_lo, x_hi), slabs: 8 (over z, y_hi).
Axes of the slice: x: 4 (x_hi: 2, x_lo: 2; x = x_hi * 2 + x_lo), y: 4 (y_hi: 2, y_lo: 2; y = y_hi * 2 + y_lo), z: 4, core: 2. Of those that a mesh axis runs over, the one named last changes fastest.
Arguments:
- pressure: float32 [64, 32, 1024, 128], P('rows', 'cols', 'slabs'), may hold values from 0.2 to 1.8
- earlier: float32 [64, 32, 1024, 128], P('rows', 'cols', 'slabs'), may hold values from 0.2 to 1.8
- speed_square: float32 [64, 32, 1024, 128], P('rows', 'cols', 'slabs'), may hold values from 0.05 to 0.3
Outputs:
- column_sum: float32 [64, 32, 1024, 128], P('rows', 'cols', 'slabs')
- pressure_end: float32 [64, 32, 1024, 128], P('rows', 'cols', 'slabs')
All inputs are finite; a program needn't handle non-finite values.
Results may differ from a plain program's by a relative error of at most 0.00002.
Values sent between devices are 32-bit elements; how exact they have to be, the bound alone decides.
A program may use at most 128 MiB of HBM per device.

v0:
```python
import jax
import jax.numpy as jnp
from jax import lax
from jax.sharding import Mesh
from jax.sharding import PartitionSpec as P

STEPS = 6
COLS = ("cols_0", "cols_1")


def extended(x, sides, width):
    edges = {}
    for axis, dim in sides:
        count, length = (lax.axis_size(axis), x.shape[dim])
        up = [(i, (i + 1) % count) for i in range(count - 1)]
        last = lax.slice_in_dim(x, length - width, length, axis=dim)
        initial = lax.slice_in_dim(x, 0, width, axis=dim)
        edges[dim] = (
            lax.ppermute(last, axis, up),
            lax.ppermute(initial, axis, [(b, a) for a, b in up]),
        )
    done = []
    for _, dim in sides:
        low, high = edges[dim]
        around = [(width, width) if d in done else (0, 0) for d in range(x.ndim)]
        x = jnp.concatenate([jnp.pad(low, around), x, jnp.pad(high, around)], axis=dim)
        done.append(dim)
    return x


def nothing_yet(x, identity):
    return jnp.zeros_like(x) + jnp.asarray(identity, x.dtype)


def prefix_by_axis(x, axes, combine, identity):
    before = start = nothing_yet(x, identity)
    so_far = x
    for axis in reversed(axes):
        count, mine = (lax.axis_size(axis), lax.axis_index(axis))
        pieces = lax.all_gather(so_far, axis)
        inside, so_far = (start, start)
        for k in range(count):
            passed = k < mine
            so_far = combine(so_far, pieces[k])
            inside = jnp.where(passed, so_far, inside)
        before = combine(inside, before)
    return before


def inner_cells(values, dims):
    for dim in dims:
        values = lax.slice_in_dim(values, 1, values.shape[dim] - 1, axis=dim)
    return values


def side_cells(values, dim, start, dims):
    others = [other for other in dims if other != dim]
    values = inner_cells(values, others)
    return lax.slice_in_dim(values, start, start + values.shape[dim] - 2, axis=dim)


def advance(padded, before, speed_square):
    middle = inner_cells(padded, (0, 1, 2))
    lower = [side_cells(padded, dim, 0, (0, 1, 2)) for dim in (0, 1, 2)]
    upper = [side_cells(padded, dim, 2, (0, 1, 2)) for dim in (0, 1, 2)]
    spread = lower[0] + upper[0] + lower[1] + upper[1] + lower[2] + upper[2] - 6.0 * middle
    return 2.0 * middle - before + speed_square * spread


def on_device(pressure, earlier, speed_square):
    for step in range(STEPS):
        padded = extended(pressure, (("rows", 0), (COLS, 1), ("slabs", 2)), 1)
        later = advance(padded, earlier, speed_square)
        earlier, pressure = (pressure, later)
    here = jnp.cumsum(pressure, axis=1)
    total = lax.slice_in_dim(here, here.shape[1] - 1, here.shape[1], axis=1)

    def add_pair(earlier_total, later_total):
        return earlier_total + later_total

    below = prefix_by_axis(total, COLS, add_pair, jnp.zeros_like(total))
    column_sum = (here + below) / (pressure.shape[1] * lax.axis_size(COLS))
    return (column_sum, pressure)


def solution(mesh):
    finer = Mesh(
        mesh.devices.reshape(mesh.shape["rows"], 2, 2, mesh.shape["slabs"]),
        ("rows", "cols_0", "cols_1", "slabs"),
    )
    placed = (
        P("rows", COLS, "slabs", None),
        P("rows", COLS, "slabs", None),
        P("rows", COLS, "slabs", None),
    )
    return jax.shard_map(
        on_device,
        mesh=finer,
        in_specs=placed,
        out_specs=(P("rows", COLS, "slabs", None), P("rows", COLS, "slabs", None)),
        check_vma=False,
    )
```

profile of v0, /device:TPU:10, one launch (start us, length us, event | category | flops | bytes accessed | tf_op | source)
XLA Modules:
  0.0 591.7 jit_solution(13634976926247008699)
XLA Ops:
  16.2 4.2 collective-permute-start.3
  24.8 4.2 collective-permute-start.4
  31.2 8.4 %constant_dynamic-update-slice_fusion.1 = f32[18,8,128,128]{3,2,1,0:T(8,128)} fusion(f32[18,8,128,128]{3,2,1,0:T(8,128)} %constant_dynamic-update-slice_fusion.2, f32[16,8,128,128]{3,2,1,0:T(8,128)} %param.3), kind=kLoop, calls=%fused_computation.169 | loop fusion | bytes 16777216
  39.6 26.4 %collective-permute-done.1 = f32[1,8,128,128]{3,2,1,0:T(8,128)S(1)} collective-permute-done((f32[1,8,128,128]{3,2,1,0:T(8,128)S(1)}, f32[1,8,128,128]{3,2,1,0:T(8,128)S(1)}, u32[]{:S(2)}, u32[]{:S(2)}) %collective-permute-start.1) | collective-permute-done | bytes 524320 | tf_op jit(solution)/shard_map/ppermute | solution.py:20
  68.3 28.4 %fusion.54 = f32[16,8,128,128]{3,2,1,0:T(8,128)} fusion(f32[16,8,128,128]{3,2,1,0:T(8,128)S(1)} %bitcast.4, f32[16,8,1,128]{3,2,1,0:T(1,128)S(1)} %collective-permute-done.5, f32[18,1,128,128]{3,2,1,0:T(8,128)} %pad.75, f32[18,8,128,128]{3,2,1,0:T(8,128)} %constant_dynamic-update-slice_fusion, f32[18,1,128,128]{3,2,1,0:T(8,128)S(1)} %pad.74, ...), kind=kLoop, calls=%fused_computation.145 | loop fusion | flops 56623104 | bytes 46530560 | tf_op jit(solution)/shard_map/add | solution.py:67
  100.3 6.3 %collective-permute-start.9 = (f32[16,1,128,128]{3,2,1,0:T(8,128)S(1)}, f32[16,1,128,128]{3,2,1,0:T(8,128)S(1)}, u32[]{:S(2)}, u32[]{:S(2)}) collective-permute-start(f32[16,1,128,128]{3,2,1,0:T(8,128)S(1)} %get-tuple-element.31), channel_id=1, source_target_pairs={{8,0},{16,8},{24,16},{9,1},{17,9},{25,17},{10,2},{18,10},{26,18},{... | collective-permute-start | bytes 3145736 | tf_op jit(solution)/shard_map/ppermute | solution.py:20
  114.8 4.2 collective-permute-start.10
  119.0 9.7 %collective-permute-done.8 = f32[16,1,128,128]{3,2,1,0:T(8,128)S(1)} collective-permute-done((f32[16,1,128,128]{3,2,1,0:T(8,128)S(1)}, f32[16,1,128,128]{3,2,1,0:T(8,128)S(1)}, u32[]{:S(2)}, u32[]{:S(2)}) %collective-permute-start.8) | collective-permute-done | bytes 1048608 | tf_op jit(solution)/shard_map/ppermute | solution.py:19
  130.6 6.6 %collective-permute-done.9 = f32[16,1,128,128]{3,2,1,0:T(8,128)S(1)} collective-permute-done((f32[16,1,128,128]{3,2,1,0:T(8,128)S(1)}, f32[16,1,128,128]{3,2,1,0:T(8,128)S(1)}, u32[]{:S(2)}, u32[]{:S(2)}) %collective-permute-start.9) | collective-permute-done | bytes 1048608 | tf_op jit(solution)/shard_map/ppermute | solution.py:20
  137.3 10.9 %collective-permute-done.6 = f32[1,8,128,128]{3,2,1,0:T(8,128)S(1)} collective-permute-done((f32[1,8,128,128]{3,2,1,0:T(8,128)S(1)}, f32[1,8,128,128]{3,2,1,0:T(8,128)S(1)}, u32[]{:S(2)}, u32[]{:S(2)}) %collective-permute-start.6) | collective-permute-done | bytes 524320 | tf_op jit(solution)/shard_map/ppermute | solution.py:19
  148.3 30.9 %fusion.44 = f32[16,8,128,128]{3,2,1,0:T(8,128)} fusion(f32[16,8,128,128]{3,2,1,0:T(8,128)} %param.5, f32[16,8,1,128]{3,2,1,0:T(1,128)S(1)} %collective-permute-done.11, f32[18,1,128,128]{3,2,1,0:T(8,128)S(1)} %pad.79, f32[18,1,128,128]{3,2,1,0:T(8,128)S(1)} %pad.78, f32[1,8,128,128]{3,2,1,0:T(8,128)S(1)} %collective-permute-done.7, ...), kind=kLoop, calls=%fused_computation.117 | loop fusion | flops 73400320 | bytes 37093376 | tf_op jit(solution)/shard_map/add | solution.py:67
  182.8 6.3 %collective-permute-start.15 = (f32[16,1,128,128]{3,2,1,0:T(8,128)S(1)}, f32[16,1,128,128]{3,2,1,0:T(8,128)S(1)}, u32[]{:S(2)}, u32[]{:S(2)}) collective-permute-start(f32[16,1,128,128]{3,2,1,0:T(8,128)S(1)} %get-tuple-element.25), channel_id=1, source_target_pairs={{8,0},{16,8},{24,16},{9,1},{17,9},{25,17},{10,2},{18,10},{26,18},{... | collective-permute-start | bytes 3145736 | tf_op jit(solution)/shard_map/ppermute | solution.py:20
  197.3 4.2 collective-permute-start.16
  210.6 12.7 %collective-permute-done.12 = f32[1,8,128,128]{3,2,1,0:T(8,128)S(1)} collective-permute-done((f32[1,8,128,128]{3,2,1,0:T(8,128)S(1)}, f32[1,8,128,128]{3,2,1,0:T(8,128)S(1)}, u32[]{:S(2)}, u32[]{:S(2)}) %collective-permute-start.12) | collective-permute-done | bytes 524320 | tf_op jit(solution)/shard_map/ppermute | solution.py:19
  223.2 31.1 %fusion.34 = f32[16,8,128,128]{3,2,1,0:T(8,128)} fusion(f32[16,8,128,128]{3,2,1,0:T(8,128)} %param.5, f32[16,8,1,128]{3,2,1,0:T(1,128)S(1)} %collective-permute-done.17, f32[18,1,128,128]{3,2,1,0:T(8,128)S(1)} %pad.83, f32[18,1,128,128]{3,2,1,0:T(8,128)S(1)} %pad.82, f32[1,8,128,128]{3,2,1,0:T(8,128)S(1)} %collective-permute-done.13, ...), kind=kLoop, calls=%fused_computation.89 | loop fusion | flops 73400320 | bytes 37093376 | tf_op jit(solution)/shard_map/add | solution.py:67
  258.0 7.1 %collective-permute-start.21 = (f32[16,1,128,128]{3,2,1,0:T(8,128)S(1)}, f32[16,1,128,128]{3,2,1,0:T(8,128)S(1)}, u32[]{:S(2)}, u32[]{:S(2)}) collective-permute-start(f32[16,1,128,128]{3,2,1,0:T(8,128)S(1)} %get-tuple-element.19), channel_id=1, source_target_pairs={{8,0},{16,8},{24,16},{9,1},{17,9},{25,17},{10,2},{18,10},{26,18},{... | collective-permute-start | bytes 3145736 | tf_op jit(solution)/shard_map/ppermute | solution.py:20
  282.9 13.4 %collective-permute-done.21 = f32[16,1,128,128]{3,2,1,0:T(8,128)S(1)} collective-permute-done((f32[16,1,128,128]{3,2,1,0:T(8,128)S(1)}, f32[16,1,128,128]{3,2,1,0:T(8,128)S(1)}, u32[]{:S(2)}, u32[]{:S(2)}) %collective-permute-start.21) | collective-permute-done | bytes 1048608 | tf_op jit(solution)/shard_map/ppermute | solution.py:20
  296.5 5.5 collective-permute-done.19
  302.0 30.9 %fusion.24 = f32[16,8,128,128]{3,2,1,0:T(8,128)} fusion(f32[16,8,128,128]{3,2,1,0:T(8,128)} %param.5, f32[16,8,1,128]{3,2,1,0:T(1,128)S(1)} %collective-permute-done.23, f32[18,1,128,128]{3,2,1,0:T(8,128)S(1)} %pad.87, f32[18,1,128,128]{3,2,1,0:T(8,128)S(1)} %pad.86, f32[1,8,128,128]{3,2,1,0:T(8,128)S(1)} %collective-permute-done.19, ...), kind=kLoop, calls=%fused_computation.61 | loop fusion | flops 73400320 | bytes 37093376 | tf_op jit(solution)/shard_map/add | solution.py:67
  337.0 5.8 collective-permute-start.27
  354.9 8.0 %collective-permute-done.26 = f32[16,1,128,128]{3,2,1,0:T(8,128)S(1)} collective-permute-done((f32[16,1,128,128]{3,2,1,0:T(8,128)S(1)}, f32[16,1,128,128]{3,2,1,0:T(8,128)S(1)}, u32[]{:S(2)}, u32[]{:S(2)}) %collective-permute-start.26) | collective-permute-done | bytes 1048608 | tf_op jit(solution)/shard_map/ppermute | solution.py:19
  364.5 4.3 collective-permute-done.27
  374.4 31.1 %fusion.14 = f32[16,8,128,128]{3,2,1,0:T(8,128)} fusion(f32[16,8,128,128]{3,2,1,0:T(8,128)} %param.5, f32[16,8,1,128]{3,2,1,0:T(1,128)S(1)} %collective-permute-done.29, f32[18,1,128,128]{3,2,1,0:T(8,128)S(1)} %pad.91, f32[18,1,128,128]{3,2,1,0:T(8,128)S(1)} %pad.90, f32[1,8,128,128]{3,2,1,0:T(8,128)S(1)} %collective-permute-done.25, ...), kind=kLoop, calls=%fused_computation.33 | loop fusion | flops 73400320 | bytes 37093376 | tf_op jit(solution)/shard_map/add | solution.py:67
  409.4 6.6 %collective-permute-start.33 = (f32[16,1,128,128]{3,2,1,0:T(8,128)S(1)}, f32[16,1,128,128]{3,2,1,0:T(8,128)S(1)}, u32[]{:S(2)}, u32[]{:S(2)}) collective-permute-start(f32[16,1,128,128]{3,2,1,0:T(8,128)S(1)} %get-tuple-element.7), channel_id=1, source_target_pairs={{8,0},{16,8},{24,16},{9,1},{17,9},{25,17},{10,2},{18,10},{26,18},{... | collective-permute-start | bytes 3145736 | tf_op jit(solution)/shard_map/ppermute | solution.py:20
  428.3 6.1 %collective-permute-done.32 = f32[16,1,128,128]{3,2,1,0:T(8,128)S(1)} collective-permute-done((f32[16,1,128,128]{3,2,1,0:T(8,128)S(1)}, f32[16,1,128,128]{3,2,1,0:T(8,128)S(1)}, u32[]{:S(2)}, u32[]{:S(2)}) %collective-permute-start.32) | collective-permute-done | bytes 1048608 | tf_op jit(solution)/shard_map/ppermute | solution.py:19
  436.0 4.9 collective-permute-done.33
  442.0 16.6 %collective-permute-done.30 = f32[1,8,128,128]{3,2,1,0:T(8,128)S(1)} collective-permute-done((f32[1,8,128,128]{3,2,1,0:T(8,128)S(1)}, f32[1,8,128,128]{3,2,1,0:T(8,128)S(1)}, u32[]{:S(2)}, u32[]{:S(2)}) %collective-permute-start.30) | collective-permute-done | bytes 524320 | tf_op jit(solution)/shard_map/ppermute | solution.py:19
  458.6 30.9 %fusion.4 = f32[16,8,128,128]{3,2,1,0:T(8,128)} fusion(f32[16,8,128,128]{3,2,1,0:T(8,128)} %param.5, f32[16,8,1,128]{3,2,1,0:T(1,128)S(1)} %collective-permute-done.35, f32[18,1,128,128]{3,2,1,0:T(8,128)S(1)} %pad.95, f32[18,1,128,128]{3,2,1,0:T(8,128)S(1)} %pad.94, f32[1,8,128,128]{3,2,1,0:T(8,128)S(1)} %collective-permute-done.31, ...), kind=kLoop, calls=%fused_computation.5 | loop fusion | flops 73400320 | bytes 37093376 | tf_op jit(solution)/shard_map/add | solution.py:67
  489.4 8.4 %fusion.81 = f32[16,8,128,128]{3,2,1,0:T(8,128)} fusion(f32[16,8,128,128]{3,2,1,0:T(8,128)} %fusion.4), kind=kOutput, calls=%fused_computation.189 | output fusion | flops 14680064 | bytes 16777216 | tf_op jit(solution)/shard_map/jit(cumsum)/reduce_window_sum | solution.py:75
  500.2 35.3 %all-gather.5.cloned.1.call-done = f32[32,1,128,128]{3,2,1,0:T(8,128)} async-done(((f32[16,1,128,128]{3,2,1,0:T(8,128)}), f32[32,1,128,128]{3,2,1,0:T(8,128)}) %all-gather.5.cloned.1.call-update) | async-done | bytes 2097168 | tf_op jit(solution)/shard_map/all_gather | solution.py:40
  538.2 35.2 %all-gather.7.cloned.1.call-done = f32[32,1,128,128]{3,2,1,0:T(8,128)} async-done(((f32[16,1,128,128]{3,2,1,0:T(8,128)}), f32[32,1,128,128]{3,2,1,0:T(8,128)}) %all-gather.7.cloned.1.call-update) | async-done | bytes 2097168 | tf_op jit(solution)/shard_map/all_gather | solution.py:40
  575.9 8.7 %add_multiply_fusion = f32[16,8,128,128]{3,2,1,0:T(8,128)} fusion(f32[16,8,128,128]{3,2,1,0:T(8,128)} %fusion.81, f32[16,128,128]{2,1,0:T(8,128)S(1)} %fusion.62), kind=kLoop, calls=%fused_computation.162 | loop fusion | flops 4194304 | bytes 17825792 | tf_op jit(solution)/shard_map/div | solution.py:82
  (99 shorter events, 123.6 us)
Async XLA Ops:
  7.2 528.4 %all-gather.5.cloned.1.call-start = ((), (), s32[]{:S(2)}) async-start(), calls=%async_computation | async-start | bytes 3145728 | tf_op jit(solution)/shard_map/all_gather | solution.py:40
  8.5 20.5 %collective-permute-start = (f32[1,8,128,128]{3,2,1,0:T(8,128)S(1)}, f32[1,8,128,128]{3,2,1,0:T(8,128)S(1)}, u32[]{:S(2)}, u32[]{:S(2)}) collective-permute-start(f32[1,8,128,128]{3,2,1,0:T(8,128)S(1)} %get-tuple-element.37), channel_id=1, source_target_pairs={{0,32},{32,64},{64,96},{1,33},{33,65},{65,97},{2,34},{34,66},{66,9... | collective-permute-start | bytes 1572872 | tf_op jit(solution)/shard_map/ppermute | solution.py:19
  12.1 54.9 %collective-permute-start.2 = (f32[16,1,128,128]{3,2,1,0:T(8,128)S(1)}, f32[16,1,128,128]{3,2,1,0:T(8,128)S(1)}, u32[]{:S(2)}, u32[]{:S(2)}) collective-permute-start(f32[16,1,128,128]{3,2,1,0:T(8,128)S(1)} %get-tuple-element.34), channel_id=1, source_target_pairs={{0,8},{8,16},{16,24},{1,9},{9,17},{17,25},{2,10},{10,18},{18,26},{... | collective-permute-start | bytes 3145736 | tf_op jit(solution)/shard_map/ppermute | solution.py:19
  16.2 51.0 %collective-permute-start.3 = (f32[16,1,128,128]{3,2,1,0:T(8,128)S(1)}, f32[16,1,128,128]{3,2,1,0:T(8,128)S(1)}, u32[]{:S(2)}, u32[]{:S(2)}) collective-permute-start(f32[16,1,128,128]{3,2,1,0:T(8,128)S(1)} %get-tuple-element.35), channel_id=1, source_target_pairs={{8,0},{16,8},{24,16},{9,1},{17,9},{25,17},{10,2},{18,10},{26,18},{... | collective-permute-start | bytes 3145736 | tf_op jit(solution)/shard_map/ppermute | solution.py:20
  20.4 45.6 %collective-permute-start.1 = (f32[1,8,128,128]{3,2,1,0:T(8,128)S(1)}, f32[1,8,128,128]{3,2,1,0:T(8,128)S(1)}, u32[]{:S(2)}, u32[]{:S(2)}) collective-permute-start(f32[1,8,128,128]{3,2,1,0:T(8,128)S(1)} %get-tuple-element.36), channel_id=1, source_target_pairs={{32,0},{64,32},{96,64},{33,1},{65,33},{97,65},{34,2},{66,34},{98,6... | collective-permute-start | bytes 1572872 | tf_op jit(solution)/shard_map/ppermute | solution.py:20
  24.8 43.5 %collective-permute-start.4 = (f32[16,8,1,128]{3,2,1,0:T(1,128)S(1)}, f32[16,8,1,128]{3,2,1,0:T(1,128)S(1)}, u32[]{:S(2)}, u32[]{:S(2)}) collective-permute-start(f32[16,8,1,128]{3,2,1,0:T(1,128)S(1)} %get-tuple-element.32), channel_id=1, source_target_pairs={{0,1},{1,2},{2,3},{3,4},{4,5},{5,6},{6,7},{8,9},{9,10},{10,11},{11... | collective-permute-start | bytes 196616 | tf_op jit(solution)/shard_map/ppermute | solution.py:19
  29.0 39.2 %collective-permute-start.5 = (f32[16,8,1,128]{3,2,1,0:T(1,128)S(1)}, f32[16,8,1,128]{3,2,1,0:T(1,128)S(1)}, u32[]{:S(2)}, u32[]{:S(2)}) collective-permute-start(f32[16,8,1,128]{3,2,1,0:T(1,128)S(1)} %get-tuple-element.33), channel_id=1, source_target_pairs={{1,0},{2,1},{3,2},{4,3},{5,4},{6,5},{7,6},{9,8},{10,9},{11,10},{12... | collective-permute-start | bytes 196616 | tf_op jit(solution)/shard_map/ppermute | solution.py:20
  98.3 30.3 %collective-permute-start.8 = (f32[16,1,128,128]{3,2,1,0:T(8,128)S(1)}, f32[16,1,128,128]{3,2,1,0:T(8,128)S(1)}, u32[]{:S(2)}, u32[]{:S(2)}) collective-permute-start(f32[16,1,128,128]{3,2,1,0:T(8,128)S(1)} %get-tuple-element.30), channel_id=1, source_target_pairs={{0,8},{8,16},{16,24},{1,9},{9,17},{17,25},{2,10},{10,18},{18,26},{... | collective-permute-start | bytes 3145736 | tf_op jit(solution)/shard_map/ppermute | solution.py:19
  100.3 36.9 %collective-permute-start.9 = (f32[16,1,128,128]{3,2,1,0:T(8,128)S(1)}, f32[16,1,128,128]{3,2,1,0:T(8,128)S(1)}, u32[]{:S(2)}, u32[]{:S(2)}) collective-permute-start(f32[16,1,128,128]{3,2,1,0:T(8,128)S(1)} %get-tuple-element.31), channel_id=1, source_target_pairs={{8,0},{16,8},{24,16},{9,1},{17,9},{25,17},{10,2},{18,10},{26,18},{... | collective-permute-start | bytes 3145736 | tf_op jit(solution)/shard_map/ppermute | solution.py:20
  107.9 40.3 %collective-permute-start.6 = (f32[1,8,128,128]{3,2,1,0:T(8,128)S(1)}, f32[1,8,128,128]{3,2,1,0:T(8,128)S(1)}, u32[]{:S(2)}, u32[]{:S(2)}) collective-permute-start(f32[1,8,128,128]{3,2,1,0:T(8,128)S(1)} %get-tuple-element.28), channel_id=1, source_target_pairs={{0,32},{32,64},{64,96},{1,33},{33,65},{65,97},{2,34},{34,66},{66,9... | collective-permute-start | bytes 1572872 | tf_op jit(solution)/shard_map/ppermute | solution.py:19
  109.8 38.4 %collective-permute-start.7 = (f32[1,8,128,128]{3,2,1,0:T(8,128)S(1)}, f32[1,8,128,128]{3,2,1,0:T(8,128)S(1)}, u32[]{:S(2)}, u32[]{:S(2)}) collective-permute-start(f32[1,8,128,128]{3,2,1,0:T(8,128)S(1)} %get-tuple-element.29), channel_id=1, source_target_pairs={{32,0},{64,32},{96,64},{33,1},{65,33},{97,65},{34,2},{66,34},{98,6... | collective-permute-start | bytes 1572872 | tf_op jit(solution)/shard_map/ppermute | solution.py:20
  114.8 22.5 %collective-permute-start.10 = (f32[16,8,1,128]{3,2,1,0:T(1,128)S(1)}, f32[16,8,1,128]{3,2,1,0:T(1,128)S(1)}, u32[]{:S(2)}, u32[]{:S(2)}) collective-permute-start(f32[16,8,1,128]{3,2,1,0:T(1,128)S(1)} %get-tuple-element.26), channel_id=1, source_target_pairs={{0,1},{1,2},{2,3},{3,4},{4,5},{5,6},{6,7},{8,9},{9,10},{10,11},{11... | collective-permute-start | bytes 196616 | tf_op jit(solution)/shard_map/ppermute | solution.py:19
  180.9 22.1 %collective-permute-start.14 = (f32[16,1,128,128]{3,2,1,0:T(8,128)S(1)}, f32[16,1,128,128]{3,2,1,0:T(8,128)S(1)}, u32[]{:S(2)}, u32[]{:S(2)}) collective-permute-start(f32[16,1,128,128]{3,2,1,0:T(8,128)S(1)} %get-tuple-element.24), channel_id=1, source_target_pairs={{0,8},{8,16},{16,24},{1,9},{9,17},{17,25},{2,10},{10,18},{18,26},{... | collective-permute-start | bytes 3145736 | tf_op jit(solution)/shard_map/ppermute | solution.py:19
  182.8 25.5 %collective-permute-start.15 = (f32[16,1,128,128]{3,2,1,0:T(8,128)S(1)}, f32[16,1,128,128]{3,2,1,0:T(8,128)S(1)}, u32[]{:S(2)}, u32[]{:S(2)}) collective-permute-start(f32[16,1,128,128]{3,2,1,0:T(8,128)S(1)} %get-tuple-element.25), channel_id=1, source_target_pairs={{8,0},{16,8},{24,16},{9,1},{17,9},{25,17},{10,2},{18,10},{26,18},{... | collective-permute-start | bytes 3145736 | tf_op jit(solution)/shard_map/ppermute | solution.py:20
  190.4 32.8 %collective-permute-start.12 = (f32[1,8,128,128]{3,2,1,0:T(8,128)S(1)}, f32[1,8,128,128]{3,2,1,0:T(8,128)S(1)}, u32[]{:S(2)}, u32[]{:S(2)}) collective-permute-start(f32[1,8,128,128]{3,2,1,0:T(8,128)S(1)} %get-tuple-element.22), channel_id=1, source_target_pairs={{0,32},{32,64},{64,96},{1,33},{33,65},{65,97},{2,34},{34,66},{66,9... | collective-permute-start | bytes 1572872 | tf_op jit(solution)/shard_map/ppermute | solution.py:19
  192.4 30.9 %collective-permute-start.13 = (f32[1,8,128,128]{3,2,1,0:T(8,128)S(1)}, f32[1,8,128,128]{3,2,1,0:T(8,128)S(1)}, u32[]{:S(2)}, u32[]{:S(2)}) collective-permute-start(f32[1,8,128,128]{3,2,1,0:T(8,128)S(1)} %get-tuple-element.23), channel_id=1, source_target_pairs={{32,0},{64,32},{96,64},{33,1},{65,33},{97,65},{34,2},{66,34},{98,6... | collective-permute-start | bytes 1572872 | tf_op jit(solution)/shard_map/ppermute | solution.py:20
  256.1 25.5 %collective-permute-start.20 = (f32[16,1,128,128]{3,2,1,0:T(8,128)S(1)}, f32[16,1,128,128]{3,2,1,0:T(8,128)S(1)}, u32[]{:S(2)}, u32[]{:S(2)}) collective-permute-start(f32[16,1,128,128]{3,2,1,0:T(8,128)S(1)} %get-tuple-element.18), channel_id=1, source_target_pairs={{0,8},{8,16},{16,24},{1,9},{9,17},{17,25},{2,10},{10,18},{18,26},{... | collective-permute-start | bytes 3145736 | tf_op jit(solution)/shard_map/ppermute | solution.py:19
  258.0 38.4 %collective-permute-start.21 = (f32[16,1,128,128]{3,2,1,0:T(8,128)S(1)}, f32[16,1,128,128]{3,2,1,0:T(8,128)S(1)}, u32[]{:S(2)}, u32[]{:S(2)}) collective-permute-start(f32[16,1,128,128]{3,2,1,0:T(8,128)S(1)} %get-tuple-element.19), channel_id=1, source_target_pairs={{8,0},{16,8},{24,16},{9,1},{17,9},{25,17},{10,2},{18,10},{26,18},{... | collective-permute-start | bytes 3145736 | tf_op jit(solution)/shard_map/ppermute | solution.py:20
  266.4 30.1 %collective-permute-start.18 = (f32[1,8,128,128]{3,2,1,0:T(8,128)S(1)}, f32[1,8,128,128]{3,2,1,0:T(8,128)S(1)}, u32[]{:S(2)}, u32[]{:S(2)}) collective-permute-start(f32[1,8,128,128]{3,2,1,0:T(8,128)S(1)} %get-tuple-element.16), channel_id=1, source_target_pairs={{0,32},{32,64},{64,96},{1,33},{33,65},{65,97},{2,34},{34,66},{66,9... | collective-permute-start | bytes 1572872 | tf_op jit(solution)/shard_map/ppermute | solution.py:19
  268.3 33.6 %collective-permute-start.19 = (f32[1,8,128,128]{3,2,1,0:T(8,128)S(1)}, f32[1,8,128,128]{3,2,1,0:T(8,128)S(1)}, u32[]{:S(2)}, u32[]{:S(2)}) collective-permute-start(f32[1,8,128,128]{3,2,1,0:T(8,128)S(1)} %get-tuple-element.17), channel_id=1, source_target_pairs={{32,0},{64,32},{96,64},{33,1},{65,33},{97,65},{34,2},{66,34},{98,6... | collective-permute-start | bytes 1572872 | tf_op jit(solution)/shard_map/ppermute | solution.py:20
  273.3 23.2 %collective-permute-start.22 = (f32[16,8,1,128]{3,2,1,0:T(1,128)S(1)}, f32[16,8,1,128]{3,2,1,0:T(1,128)S(1)}, u32[]{:S(2)}, u32[]{:S(2)}) collective-permute-start(f32[16,8,1,128]{3,2,1,0:T(1,128)S(1)} %get-tuple-element.14), channel_id=1, source_target_pairs={{0,1},{1,2},{2,3},{3,4},{4,5},{5,6},{6,7},{8,9},{9,10},{10,11},{11... | collective-permute-start | bytes 196616 | tf_op jit(solution)/shard_map/ppermute | solution.py:19
  334.5 28.4 %collective-permute-start.26 = (f32[16,1,128,128]{3,2,1,0:T(8,128)S(1)}, f32[16,1,128,128]{3,2,1,0:T(8,128)S(1)}, u32[]{:S(2)}, u32[]{:S(2)}) collective-permute-start(f32[16,1,128,128]{3,2,1,0:T(8,128)S(1)} %get-tuple-element.12), channel_id=1, source_target_pairs={{0,8},{8,16},{16,24},{1,9},{9,17},{17,25},{2,10},{10,18},{18,26},{... | collective-permute-start | bytes 3145736 | tf_op jit(solution)/shard_map/ppermute | solution.py:19
  337.0 31.8 %collective-permute-start.27 = (f32[16,1,128,128]{3,2,1,0:T(8,128)S(1)}, f32[16,1,128,128]{3,2,1,0:T(8,128)S(1)}, u32[]{:S(2)}, u32[]{:S(2)}) collective-permute-start(f32[16,1,128,128]{3,2,1,0:T(8,128)S(1)} %get-tuple-element.13), channel_id=1, source_target_pairs={{8,0},{16,8},{24,16},{9,1},{17,9},{25,17},{10,2},{18,10},{26,18},{... | collective-permute-start | bytes 3145736 | tf_op jit(solution)/shard_map/ppermute | solution.py:20
  344.1 26.5 %collective-permute-start.24 = (f32[1,8,128,128]{3,2,1,0:T(8,128)S(1)}, f32[1,8,128,128]{3,2,1,0:T(8,128)S(1)}, u32[]{:S(2)}, u32[]{:S(2)}) collective-permute-start(f32[1,8,128,128]{3,2,1,0:T(8,128)S(1)} %get-tuple-element.10), channel_id=1, source_target_pairs={{0,32},{32,64},{64,96},{1,33},{33,65},{65,97},{2,34},{34,66},{66,9... | collective-permute-start | bytes 1572872 | tf_op jit(solution)/shard_map/ppermute | solution.py:19
  346.0 28.4 %collective-permute-start.25 = (f32[1,8,128,128]{3,2,1,0:T(8,128)S(1)}, f32[1,8,128,128]{3,2,1,0:T(8,128)S(1)}, u32[]{:S(2)}, u32[]{:S(2)}) collective-permute-start(f32[1,8,128,128]{3,2,1,0:T(8,128)S(1)} %get-tuple-element.11), channel_id=1, source_target_pairs={{32,0},{64,32},{96,64},{33,1},{65,33},{97,65},{34,2},{66,34},{98,6... | collective-permute-start | bytes 1572872 | tf_op jit(solution)/shard_map/ppermute | solution.py:20
  351.0 17.9 %collective-permute-start.28 = (f32[16,8,1,128]{3,2,1,0:T(1,128)S(1)}, f32[16,8,1,128]{3,2,1,0:T(1,128)S(1)}, u32[]{:S(2)}, u32[]{:S(2)}) collective-permute-start(f32[16,8,1,128]{3,2,1,0:T(1,128)S(1)} %get-tuple-element.8), channel_id=1, source_target_pairs={{0,1},{1,2},{2,3},{3,4},{4,5},{5,6},{6,7},{8,9},{9,10},{10,11},{11... | collective-permute-start | bytes 196616 | tf_op jit(solution)/shard_map/ppermute | solution.py:19
  407.3 27.1 %collective-permute-start.32 = (f32[16,1,128,128]{3,2,1,0:T(8,128)S(1)}, f32[16,1,128,128]{3,2,1,0:T(8,128)S(1)}, u32[]{:S(2)}, u32[]{:S(2)}) collective-permute-start(f32[16,1,128,128]{3,2,1,0:T(8,128)S(1)} %get-tuple-element.6), channel_id=1, source_target_pairs={{0,8},{8,16},{16,24},{1,9},{9,17},{17,25},{2,10},{10,18},{18,26},{... | collective-permute-start | bytes 3145736 | tf_op jit(solution)/shard_map/ppermute | solution.py:19
  409.4 31.5 %collective-permute-start.33 = (f32[16,1,128,128]{3,2,1,0:T(8,128)S(1)}, f32[16,1,128,128]{3,2,1,0:T(8,128)S(1)}, u32[]{:S(2)}, u32[]{:S(2)}) collective-permute-start(f32[16,1,128,128]{3,2,1,0:T(8,128)S(1)} %get-tuple-element.7), channel_id=1, source_target_pairs={{8,0},{16,8},{24,16},{9,1},{17,9},{25,17},{10,2},{18,10},{26,18},{... | collective-permute-start | bytes 3145736 | tf_op jit(solution)/shard_map/ppermute | solution.py:20
  417.3 41.3 %collective-permute-start.30 = (f32[1,8,128,128]{3,2,1,0:T(8,128)S(1)}, f32[1,8,128,128]{3,2,1,0:T(8,128)S(1)}, u32[]{:S(2)}, u32[]{:S(2)}) collective-permute-start(f32[1,8,128,128]{3,2,1,0:T(8,128)S(1)} %get-tuple-element.4), channel_id=1, source_target_pairs={{0,32},{32,64},{64,96},{1,33},{33,65},{65,97},{2,34},{34,66},{66,9... | collective-permute-start | bytes 1572872 | tf_op jit(solution)/shard_map/ppermute | solution.py:19
  419.2 39.4 %collective-permute-start.31 = (f32[1,8,128,128]{3,2,1,0:T(8,128)S(1)}, f32[1,8,128,128]{3,2,1,0:T(8,128)S(1)}, u32[]{:S(2)}, u32[]{:S(2)}) collective-permute-start(f32[1,8,128,128]{3,2,1,0:T(8,128)S(1)} %get-tuple-element.5), channel_id=1, source_target_pairs={{32,0},{64,32},{96,64},{33,1},{65,33},{97,65},{34,2},{66,34},{98,6... | collective-permute-start | bytes 1572872 | tf_op jit(solution)/shard_map/ppermute | solution.py:20
  424.7 16.3 %collective-permute-start.34 = (f32[16,8,1,128]{3,2,1,0:T(1,128)S(1)}, f32[16,8,1,128]{3,2,1,0:T(1,128)S(1)}, u32[]{:S(2)}, u32[]{:S(2)}) collective-permute-start(f32[16,8,1,128]{3,2,1,0:T(1,128)S(1)} %get-tuple-element.2), channel_id=1, source_target_pairs={{0,1},{1,2},{2,3},{3,4},{4,5},{5,6},{6,7},{8,9},{9,10},{10,11},{11... | collective-permute-start | bytes 196616 | tf_op jit(solution)/shard_map/ppermute | solution.py:19
  500.1 73.3 %all-gather.7.cloned.1.call-start = ((), (), s32[]{:S(2)}) async-start(), calls=%async_computation.1 | async-start | bytes 3145728 | tf_op jit(solution)/shard_map/all_gather | solution.py:40
  (10 other events, 134.9 us)
Sparse Core Ops, SparseCore 0:
  500.3 35.2 all-gather.4
  538.4 35.0 all-gather.6
where the time goes:
time: 600 us; the launch traced here: 592 us
  waiting for transfers between devices  214 us (36%)
  other arithmetic  206 us (34%)
  starting transfers between devices  117 us (20%)
  local copies, waits for them, and re-layouts  40.5 us (7%)
  between operations  14.9 us (2%)
    add x6, other arithmetic, advance(): return 2.0 * middle - before + speed_square * spread  183 us
    ppermute x18, waiting for transfers between devices, extended(): lax.ppermute(initial, axis, [(b, a) for a, b in up])  73.7 us
    all_gather x2, waiting for transfers between devices, prefix_by_axis(): pieces = lax.all_gather(so_far, axis)  70.5 us
    ppermute x18, waiting for transfers between devices, extended(): lax.ppermute(last, axis, up)  69.3 us
    ppermute x18, starting transfers between devices, extended(): lax.ppermute(initial, axis, [(b, a) for a, b in up])  66.8 us
    ppermute x18, starting transfers between devices, extended(): lax.ppermute(last, axis, up)  50.2 us
    slice x17, local copies, waits for them, and re-layouts, extended(): last = lax.slice_in_dim(x, length - width, length, axis=dim)  24.4 us
  transfers between devices with their start and end apart: 38, of which 21 were waited for; matrix products, arithmetic and copies ran while one was open for 5% of the time, Pallas kernels for 0%

commit v1 on v0

v1 whole, which is shorter than its diff:
```python
import jax
import jax.numpy as jnp
from jax import lax
from jax.experimental import pallas as pl
from jax.experimental.pallas import tpu as pltpu
from jax.sharding import Mesh
from jax.sharding import PartitionSpec as P

MESH = pl.DeviceIdType.MESH
AXES = ("x_lo", "core", "y_lo", "x_hi", "z", "y_hi")
STEPS = 6
ROWS, CELLS, DEPTH, MEMBERS = 16, 8, 128, 128
CHUNKS = ROWS // 2
PAD = 8
PIECE = 32
LAG = 1


def inner_place(k, j):
    return 4 + 2 * k + j - lax.div(k, CHUNKS - 1) * (1 + 2 * j)


def where_am_i():
    at = {axis: lax.axis_index(axis) for axis in AXES}
    col = at["y_lo"] * 2 + at["x_hi"]
    row = at["x_lo"] * 2 + at["core"]
    slab = at["z"] * 2 + at["y_hi"]
    return at, row, col, slab


def step_to(index, by, axes):
    there = index + by + 8
    return {axes[0]: lax.rem(lax.div(there, 2), 4 if axes[0] == "z" else 2), axes[1]: lax.rem(there, 2)}


def steps_kernel(
    pressure, earlier, speed, end, before,
    field, c, face, halo, passing, total, across, both, below,
    load_sem, send_x, recv_x, send_y, recv_y, send_z, recv_z, pass_send, pass_recv,
    end_sem, across_send, across_recv, both_send, both_recv,
):
    at, row, col, slab = where_am_i()
    col_lo, col_hi = step_to(col, -1, ("y_lo", "x_hi")), step_to(col, 1, ("y_lo", "x_hi"))
    row_lo, row_hi = step_to(row, -1, ("x_lo", "core")), step_to(row, 1, ("x_lo", "core"))
    slab_lo, slab_hi = step_to(slab, -1, ("z", "y_hi")), step_to(slab, 1, ("z", "y_hi"))
    other_y = {"y_lo": 1 - at["y_lo"]}
    other_x = {"x_hi": 1 - at["x_hi"]}
    has_col = (col > 0, col < 3)
    has_row = (row > 0, row < 3)
    has_slab = (slab > 0, slab < 7)
    to_col, to_row, to_slab = (col_lo, col_hi), (row_lo, row_hi), (slab_lo, slab_hi)
    relay = (col == 0) | (col == 3)
    cells, depth = pl.ds(1, CELLS), pl.ds(PAD, DEPTH)

    def remote(src, dst, send, recv, device):
        return pltpu.make_async_remote_copy(
            src_ref=src, dst_ref=dst, send_sem=send, recv_sem=recv, device_id=device, device_id_type=MESH
        )

    def load(ref, which, k, j):
        y = (15 - k) if j else k
        if which == 2:
            dst = c.at[2 * k + j]
        else:
            dst = field.at[which, 2 + 2 * k + j, cells, depth, :]
        return pltpu.make_async_copy(ref.at[y], dst, load_sem.at[which, k])

    def wait_load(which, k):
        if which == 2:
            dst = c.at[pl.ds(2 * k, 2)]
        else:
            dst = field.at[which, pl.ds(2 + 2 * k, 2), cells, depth, :]
        pltpu.make_async_copy(dst, dst, load_sem.at[which, k]).wait()

    for which, ref in enumerate((pressure, earlier, speed)):
        for j in (0, 1):
            lax.fori_loop(0, CHUNKS, lambda k, _: (load(ref, which, k, j).start(), 0)[1], 0)

    barrier = pltpu.get_barrier_semaphore()
    count = jnp.int32(1)
    for has, to in ((has_col, to_col), (has_row, to_row), (has_slab, to_slab)):
        for side in (0, 1):
            @pl.when(has[side])
            def _():
                pl.semaphore_signal(barrier, inc=1, device_id=to[side], device_id_type=MESH)
            count = count + has[side].astype(jnp.int32)
    pl.semaphore_signal(barrier, inc=1, device_id=other_y, device_id_type=MESH)
    pl.semaphore_wait(barrier, count)

    zeros = jnp.zeros((DEPTH, MEMBERS), jnp.float32)
    for side in (0, 1):
        @pl.when(jnp.logical_not(has_col[side]))
        def _():
            def clear(i, _):
                for slot in (0, 1):
                    field[slot, 2 + i, side * (CELLS + 1), PAD:PAD + DEPTH, :] = zeros
                return 0
            lax.fori_loop(0, ROWS, clear, 0)

        @pl.when(jnp.logical_not(has_row[side]))
        def _():
            def clear(i, _):
                for slot in (0, 1):
                    field[slot, side, 1 + i, PAD:PAD + DEPTH, :] = zeros
                return 0
            lax.fori_loop(0, CELLS, clear, 0)

        @pl.when(jnp.logical_not(has_slab[side]))
        def _():
            def clear(i, _):
                for slot in (0, 1):
                    halo[slot, side, i] = zeros[:CELLS]
                return 0
            lax.fori_loop(0, ROWS, clear, 0)

    def x_pieces(slot, k, side):
        own, theirs = (CELLS, 0) if side else (1, CELLS + 1)
        places = pl.ds(2 + 2 * k, 2)
        return own, theirs, places

    def send_faces(t, k):
        slot, third = lax.rem(t, 2), lax.rem(t, 3)
        for side in (1, 0):
            own, theirs, places = x_pieces(slot, k, side)
            send, recv = send_x.at[side, slot, k], recv_x.at[1 - side, slot, k]
            middle = col == (1 if side else 2)

            @pl.when(has_col[side] & jnp.logical_not(middle))
            def _():
                remote(
                    field.at[slot, places, own, depth, :], field.at[slot, places, theirs, depth, :],
                    send, recv, to_col[side],
                ).start()

            @pl.when(middle)
            def _():
                remote(
                    field.at[slot, 3 + 2 * k, own, depth, :], passing.at[third, k],
                    send, pass_recv.at[third, k], other_y,
                ).start()
                remote(
                    field.at[slot, 2 + 2 * k, own, depth, :], field.at[slot, 2 + 2 * k, theirs, depth, :],
                    send, recv, to_col[side],
                ).start()

        for side in (0, 1):
            @pl.when(has_row[side] & (k == 0))
            def _():
                remote(
                    field.at[slot, 2 + side, cells, depth, :], field.at[slot, 1 - side, cells, depth, :],
                    send_y.at[side, slot], recv_y.at[1 - side, slot], to_row[side],
                ).start()

            @pl.when(has_slab[side])
            def _():
                remote(
                    face.at[slot, side, pl.ds(2 * k, 2)], halo.at[slot, 1 - side, pl.ds(2 * k, 2)],
                    send_z.at[side, slot, k], recv_z.at[1 - side, slot, k], to_slab[side],
                ).start()

    def wait_sent(slot, k):
        for side in (0, 1):
            @pl.when(has_col[side])
            def _():
                own, theirs, places = x_pieces(slot, k, side)
                ref = field.at[slot, places, own, depth, :]
                remote(ref, ref, send_x.at[side, slot, k], recv_x.at[side, slot, k], other_y).wait_send()

            @pl.when(has_row[side] & (k == 0))
            def _():
                ref = field.at[slot, 2 + side, cells, depth, :]
                remote(ref, ref, send_y.at[side, slot], recv_y.at[side, slot], other_y).wait_send()

            @pl.when(has_slab[side])
            def _():
                ref = face.at[slot, side, pl.ds(2 * k, 2)]
                remote(ref, ref, send_z.at[side, slot, k], recv_z.at[side, slot, k], other_y).wait_send()

    def wait_faces(slot, k):
        for side in (0, 1):
            @pl.when(has_row[side] & (k == 0))
            def _():
                ref = field.at[slot, side, cells, depth, :]
                remote(ref, ref, send_y.at[side, slot], recv_y.at[side, slot], other_y).wait_recv()

            @pl.when(has_slab[side])
            def _():
                ref = halo.at[slot, side, pl.ds(2 * k, 2)]
                remote(ref, ref, send_z.at[side, slot, k], recv_z.at[side, slot, k], other_y).wait_recv()

        for side in (0, 1):
            @pl.when(has_col[side])
            def _():
                ref = field.at[slot, pl.ds(2 + 2 * k, 2), side * (CELLS + 1), depth, :]
                remote(ref, ref, send_x.at[side, slot, k], recv_x.at[side, slot, k], other_y).wait_recv()

    def wait_passed(t, k):
        @pl.when(relay)
        def _():
            third = lax.rem(t, 3)
            ref = passing.at[third, k]
            remote(ref, ref, pass_send.at[third, k], pass_recv.at[third, k], other_y).wait_send()

    def pass_on(message):
        t, k = lax.div(message, CHUNKS), lax.rem(message, CHUNKS)
        slot, third = lax.rem(t, 2), lax.rem(t, 3)

        @pl.when(t >= 1)
        def _():
            wait_passed(t - 1, k)

        @pl.when(relay)
        def _():
            side = 1 - at["y_lo"]
            copy = remote(
                passing.at[third, k], field.at[slot, 3 + 2 * k, side * (CELLS + 1), depth, :],
                pass_send.at[third, k], recv_x.at[side, slot, k], other_x,
            )
            remote(
                passing.at[third, k], passing.at[third, k],
                pass_send.at[third, k], pass_recv.at[third, k], other_y,
            ).wait_recv()
            copy.start()

    def advance(slot, k, last):
        for j in (0, 1):
            place = 2 + 2 * k + j
            inner = inner_place(k, j)
            low, high = halo[slot, 0, 2 * k + j], halo[slot, 1, 2 * k + j]
            for x in range(CELLS):
                field[slot, place, 1 + x, PAD - 1:PAD, :] = low[x:x + 1]
                field[slot, place, 1 + x, PAD + DEPTH:PAD + DEPTH + 1, :] = high[x:x + 1]
            if last:
                total[2 * k + j] = zeros

            def one(i, _):
                x = i + 1
                for z in range(0, DEPTH, PIECE):
                    here = pl.ds(PAD + z, PIECE)
                    middle = field[slot, place, x, here, :]
                    spread = field[slot, place - 2, x, here, :] + field[slot, inner, x, here, :]
                    spread = spread + field[slot, place, x - 1, here, :]
                    spread = spread + field[slot, place, x + 1, here, :]
                    spread = spread + field[slot, place, x, pl.ds(PAD + z - 1, PIECE), :]
                    spread = spread + field[slot, place, x, pl.ds(PAD + z + 1, PIECE), :]
                    spread = spread - 6.0 * middle
                    new = (
                        2.0 * middle - field[1 - slot, place, x, here, :]
                        + c[2 * k + j, i, pl.ds(z, PIECE), :] * spread
                    )
                    field[1 - slot, place, x, here, :] = new
                    if last:
                        total[2 * k + j, pl.ds(z, PIECE), :] += new
                return 0

            lax.fori_loop(0, CELLS, one, 0)

    def take_ends(slot, k):
        for j in (0, 1):
            place = 2 + 2 * k + j
            for x in range(CELLS):
                face[slot, 0, 2 * k + j, x:x + 1, :] = field[slot, place, 1 + x, PAD:PAD + 1, :]
                face[slot, 1, 2 * k + j, x:x + 1, :] = field[slot, place, 1 + x, PAD + DEPTH - 1:PAD + DEPTH, :]

    def start(k, _):
        wait_load(0, k)
        take_ends(0, k)
        send_faces(jnp.int32(0), k)

        @pl.when(k >= LAG)
        def _():
            pass_on(k - LAG)
        return 0

    lax.fori_loop(0, CHUNKS, start, 0)

    def main(n, _):
        t, k = lax.div(n, CHUNKS), lax.rem(n, CHUNKS)
        slot = lax.rem(t, 2)

        @pl.when(n < CHUNKS)
        def _():
            wait_load(1, k)
            wait_load(2, k)

        wait_faces(slot, k)

        @pl.when(n >= CHUNKS)
        def _():
            wait_sent(1 - slot, k)

        advance(slot, k, False)
        take_ends(1 - slot, k)
        send_faces(t + 1, k)
        pass_on(n + CHUNKS - LAG)
        return 0

    lax.fori_loop(0, CHUNKS * (STEPS - 1), main, 0)
    for message in range(CHUNKS * STEPS - LAG, CHUNKS * STEPS):
        pass_on(jnp.int32(message))

    final = STEPS % 2

    def chunk(k):
        return pl.ds(2 * k, 2)

    def send_across(k):
        return remote(total.at[chunk(k)], across.at[chunk(k)], across_send.at[k], across_recv.at[k], other_x)

    def send_both(k):
        return remote(both.at[chunk(k)], below.at[chunk(k)], both_send.at[k], both_recv.at[k], other_y)

    def add_up(k):
        @pl.when(col < 2)
        def _():
            send_across(k).wait_recv()
            for j in (0, 1):
                both[2 * k + j] = total[2 * k + j] + across[2 * k + j]
            send_both(k).start()

    def out(k, j):
        y = (15 - k) if j else k
        return pltpu.make_async_copy(field.at[final, 2 + 2 * k + j, cells, depth, :], end.at[y], end_sem.at[k])

    def finish(k, _):
        wait_faces(1 - final, k)
        wait_sent(final, k)
        advance(1 - final, k, True)

        @pl.when(col < 3)
        def _():
            send_across(k).start()
        for j in (0, 1):
            out(k, j).start()

        @pl.when(k >= 1)
        def _():
            add_up(k - 1)
        return 0

    lax.fori_loop(0, CHUNKS, finish, 0)
    add_up(CHUNKS - 1)

    def collect(k, _):
        for j in (0, 1):
            @pl.when(col == 0)
            def _():
                before[2 * k + j] = zeros

        @pl.when(col == 1)
        def _():
            for j in (0, 1):
                before[2 * k + j] = across[2 * k + j]

        @pl.when(col == 2)
        def _():
            send_both(k).wait_recv()
            for j in (0, 1):
                before[2 * k + j] = below[2 * k + j]

        @pl.when(col == 3)
        def _():
            send_across(k).wait_recv()
            send_both(k).wait_recv()
            for j in (0, 1):
                before[2 * k + j] = below[2 * k + j] + across[2 * k + j]

        @pl.when(col < 3)
        def _():
            send_across(k).wait_send()

        @pl.when(col < 2)
        def _():
            send_both(k).wait_send()

        wait_sent(1 - final, k)
        wait_passed(STEPS - 1, k)
        done = field.at[final, pl.ds(2 + 2 * k, 2), cells, depth, :]
        pltpu.make_async_copy(done, done, end_sem.at[k]).wait()
        return 0

    lax.fori_loop(0, CHUNKS, collect, 0)


def sums_kernel(end, before, column_sum, pressure_end):
    so_far = before[0]
    for x in range(CELLS):
        here = end[0, x]
        so_far = so_far + here
        column_sum[0, x] = so_far * (1.0 / 32.0)
        pressure_end[0, x] = here


def on_device(pressure, earlier, speed_square):
    whole = pl.BlockSpec(memory_space=pl.ANY)
    dma = pltpu.SemaphoreType.DMA
    f32 = jnp.float32
    block = (ROWS, CELLS, DEPTH, MEMBERS)
    plane = (ROWS, DEPTH, MEMBERS)
    end, before = pl.pallas_call(
        steps_kernel,
        out_shape=(jax.ShapeDtypeStruct(block, f32), jax.ShapeDtypeStruct(plane, f32)),
        in_specs=[whole] * 3,
        out_specs=(whole, pl.BlockSpec(memory_space=pltpu.VMEM)),
        scratch_shapes=[
            pltpu.VMEM((2, ROWS + 2, CELLS + 2, DEPTH + 2 * PAD, MEMBERS), f32),
            pltpu.VMEM(block, f32),
            pltpu.VMEM((2, 2, ROWS, CELLS, MEMBERS), f32),
            pltpu.VMEM((2, 2, ROWS, CELLS, MEMBERS), f32),
            pltpu.VMEM((3, CHUNKS, DEPTH, MEMBERS), f32),
            pltpu.VMEM(plane, f32),
            pltpu.VMEM(plane, f32),
            pltpu.VMEM(plane, f32),
            pltpu.VMEM(plane, f32),
            dma((3, CHUNKS)),
            dma((2, 2, CHUNKS)), dma((2, 2, CHUNKS)),
            dma((2, 2)), dma((2, 2)),
            dma((2, 2, CHUNKS)), dma((2, 2, CHUNKS)),
            dma((3, CHUNKS)), dma((3, CHUNKS)),
            dma((CHUNKS,)),
            dma((CHUNKS,)), dma((CHUNKS,)),
            dma((CHUNKS,)), dma((CHUNKS,)),
        ],
        compiler_params=pltpu.CompilerParams(
            collective_id=0, has_side_effects=True, vmem_limit_bytes=56 * 1024 * 1024
        ),
        name="steps",
    )(pressure, earlier, speed_square)

    row = pl.BlockSpec((1, CELLS, DEPTH, MEMBERS), lambda y: (y, 0, 0, 0))

    def place(y):
        late = lax.div(y, ROWS // 2)
        return ((1 - late) * 2 * y + late * (2 * (15 - y) + 1), 0, 0)

    return pl.pallas_call(
        sums_kernel,
        grid=(ROWS,),
        out_shape=(jax.ShapeDtypeStruct(block, f32), jax.ShapeDtypeStruct(block, f32)),
        in_specs=[row, pl.BlockSpec((1, DEPTH, MEMBERS), place)],
        out_specs=(row, row),
        name="sums",
    )(end, before)


def solution(mesh):
    finer = Mesh(mesh.devices.reshape(2, 2, 2, 2, 4, 2), AXES)
    placed = P(("x_lo", "core"), ("y_lo", "x_hi"), ("z", "y_hi"), None)
    return jax.shard_map(
        on_device,
        mesh=finer,
        in_specs=(placed,) * 3,
        out_specs=(placed, placed),
        check_vma=False,
    )
```

time: 600 us -> 294 us (0.49); the launches traced: 592 us -> 294 us
  Pallas kernels: 0 us -> 293 us
  waiting for transfers between devices: 214 us -> 0 us
  other arithmetic: 206 us -> 0 us
  starting transfers between devices: 117 us -> 0 us
  local copies, waits for them, and re-layouts: 40.5 us -> 0 us
  between operations: 14.9 us -> 0.64 us
    pallas_call x0 -> x2, Pallas kernels: none -> 293 us  [the longest x1 280 us: on_device(): pl.pallas_call(steps_kernel, out_shape=(jax.ShapeDtypeStruct(block, f32),...]
    add x8 -> x0, other arithmetic: 188 us -> none  [the longest x6 183 us: advance(): return 2.0 * middle - before + speed_square * spread]
    ppermute x36 -> x0, waiting for transfers between devices: 143 us -> none  [the longest x18 73.7 us: extended(): lax.ppermute(initial, axis, [(b, a) for a, b in up])]
    ppermute x36 -> x0, starting transfers between devices: 117 us -> none  [the longest x18 66.8 us: extended(): lax.ppermute(initial, axis, [(b, a) for a, b in up])]
    all_gather x2 -> x0, waiting for transfers between devices: 70.5 us -> none  [prefix_by_axis(): pieces = lax.all_gather(so_far, axis)]
    slice x19 -> x0, local copies, waits for them, and re-layouts: 28 us -> none  [the longest x17 24.4 us: extended(): last = lax.slice_in_dim(x, length - width, length, axis=dim)]
    unnamed x10 -> x0, local copies, waits for them, and re-layouts: 9.38 us -> none
    div x1 -> x0, other arithmetic: 8.68 us -> none  [on_device(): column_sum = (here + below) / (pressure.shape[1] * lax.axis_size(COLS))]
  transfers between devices with their start and end apart: 38 -> 0, of which waited for: 21 -> 0; matrix products, arithmetic and copies ran while one was open for 5% -> 0% of each run, Pallas kernels for 0% -> 0%
where the time goes in v1:
time: 294 us
  Pallas kernels  293 us (100%)
    pallas_call x1, Pallas kernels, on_device(): pl.pallas_call(steps_kernel, out_shape=(jax.ShapeDtypeStruct(block, f32),...  280 us
    pallas_call x1, Pallas kernels, on_device(): pl.pallas_call(sums_kernel, grid=(ROWS,), out_shape=(jax.ShapeDtypeStruct...  13.5 us

profile of v1, /device:TPU:10, one launch (start us, length us, event | category | flops | bytes accessed | tf_op | source)
XLA Modules:
  0.0 293.8 jit_solution(14898720998455216392)
XLA Ops:
  0.6 279.7 %steps.1 = (f32[16,8,128,128]{3,2,1,0:T(8,128)}, f32[16,128,128]{2,1,0:T(8,128)}) custom-call(f32[16,8,128,128]{3,2,1,0:T(8,128)} %pressure.1, f32[16,8,128,128]{3,2,1,0:T(8,128)} %earlier.1, f32[16,8,128,128]{3,2,1,0:T(8,128)} %speed.1), custom_call_target="tpu_custom_call" | custom-call | tf_op jit(solution)/shard_map/steps/pallas_call | solution.py:400
  280.3 13.5 %sums.1 = (f32[16,8,128,128]{3,2,1,0:T(8,128)}, f32[16,8,128,128]{3,2,1,0:T(8,128)}) custom-call(f32[16,8,128,128]{3,2,1,0:T(8,128)} %get-tuple-element.4.end, f32[16,128,128]{2,1,0:T(8,128)} %get-tuple-element.5.before), custom_call_target="tpu_custom_call" | custom-call | tf_op jit(solution)/shard_map/sums/pallas_call | solution.py:436

commit v2 on v1

--- a/solution.py
+++ b/solution.py
@@ -14,6 +14,7 @@
 PAD = 8
 PIECE = 32
 LAG = 1
+LAG_UP = 1
 
 
 def inner_place(k, j):
@@ -34,10 +35,10 @@
 
 
 def steps_kernel(
-    pressure, earlier, speed, end, before,
-    field, c, face, halo, passing, total, across, both, below,
+    pressure, earlier, speed, end, below, before,
+    field, c, face, halo, passing, total, both,
     load_sem, send_x, recv_x, send_y, recv_y, send_z, recv_z, pass_send, pass_recv,
-    end_sem, across_send, across_recv, both_send, both_recv,
+    up_send, up_recv, across_send, across_recv,
 ):
     at, row, col, slab = where_am_i()
     col_lo, col_hi = step_to(col, -1, ("y_lo", "x_hi")), step_to(col, 1, ("y_lo", "x_hi"))
@@ -85,7 +86,6 @@
                 pl.semaphore_signal(barrier, inc=1, device_id=to[side], device_id_type=MESH)
             count = count + has[side].astype(jnp.int32)
     pl.semaphore_signal(barrier, inc=1, device_id=other_y, device_id_type=MESH)
-    pl.semaphore_wait(barrier, count)
 
     zeros = jnp.zeros((DEPTH, MEMBERS), jnp.float32)
     for side in (0, 1):
@@ -112,6 +112,8 @@
                     halo[slot, side, i] = zeros[:CELLS]
                 return 0
             lax.fori_loop(0, ROWS, clear, 0)
+
+    pl.semaphore_wait(barrier, count)
 
     def x_pieces(slot, k, side):
         own, theirs = (CELLS, 0) if side else (1, CELLS + 1)
@@ -248,9 +250,11 @@
                         2.0 * middle - field[1 - slot, place, x, here, :]
                         + c[2 * k + j, i, pl.ds(z, PIECE), :] * spread
                     )
-                    field[1 - slot, place, x, here, :] = new
                     if last:
+                        end[2 * k + j, i, pl.ds(z, PIECE), :] = new
                         total[2 * k + j, pl.ds(z, PIECE), :] += new
+                    else:
+                        field[1 - slot, place, x, here, :] = new
                 return 0
 
             lax.fori_loop(0, CELLS, one, 0)
@@ -300,95 +304,106 @@
         pass_on(jnp.int32(message))
 
     final = STEPS % 2
+    early = at["y_lo"] == 0
 
     def chunk(k):
         return pl.ds(2 * k, 2)
 
-    def send_across(k):
-        return remote(total.at[chunk(k)], across.at[chunk(k)], across_send.at[k], across_recv.at[k], other_x)
-
-    def send_both(k):
-        return remote(both.at[chunk(k)], below.at[chunk(k)], both_send.at[k], both_recv.at[k], other_y)
-
-    def add_up(k):
-        @pl.when(col < 2)
-        def _():
-            send_across(k).wait_recv()
+    def send_up(k):
+        return remote(total.at[chunk(k)], below.at[chunk(k)], up_send.at[k], up_recv.at[k], other_y)
+
+    def send_across(k, source):
+        return remote(source.at[chunk(k)], before.at[chunk(k)], across_send.at[k], across_recv.at[k], other_x)
+
+    def from_below(k):
+        @pl.when(jnp.logical_not(early))
+        def _():
+            send_up(k).wait_recv()
+
+        @pl.when(col == 2)
+        def _():
             for j in (0, 1):
-                both[2 * k + j] = total[2 * k + j] + across[2 * k + j]
-            send_both(k).start()
-
-    def out(k, j):
-        y = (15 - k) if j else k
-        return pltpu.make_async_copy(field.at[final, 2 + 2 * k + j, cells, depth, :], end.at[y], end_sem.at[k])
+                both[2 * k + j] = total[2 * k + j] + below[2 * k + j]
+            send_across(k, both).start()
+
+        @pl.when(col == 3)
+        def _():
+            send_across(k, below).start()
 
     def finish(k, _):
         wait_faces(1 - final, k)
+        advance(1 - final, k, True)
+
+        @pl.when(early)
+        def _():
+            send_up(k).start()
+
+        @pl.when(col == 0)
+        def _():
+            send_across(k, total).start()
+
+        @pl.when(k >= LAG_UP)
+        def _():
+            from_below(k - LAG_UP)
+        return 0
+
+    lax.fori_loop(0, CHUNKS, finish, 0)
+    for k in range(CHUNKS - LAG_UP, CHUNKS):
+        from_below(k)
+
+    def settle(k, _):
+        @pl.when(col == 0)
+        def _():
+            for j in (0, 1):
+                before[2 * k + j] = zeros
+
+        @pl.when(early)
+        def _():
+            for j in (0, 1):
+                below[2 * k + j] = zeros
+            send_up(k).wait_send()
+
+        @pl.when(col != 1)
+        def _():
+            send_across(k, total).wait_send()
         wait_sent(final, k)
-        advance(1 - final, k, True)
-
-        @pl.when(col < 3)
-        def _():
-            send_across(k).start()
-        for j in (0, 1):
-            out(k, j).start()
-
-        @pl.when(k >= 1)
-        def _():
-            add_up(k - 1)
-        return 0
-
-    lax.fori_loop(0, CHUNKS, finish, 0)
-    add_up(CHUNKS - 1)
-
-    def collect(k, _):
-        for j in (0, 1):
-            @pl.when(col == 0)
-            def _():
-                before[2 * k + j] = zeros
-
-        @pl.when(col == 1)
-        def _():
-            for j in (0, 1):
-                before[2 * k + j] = across[2 * k + j]
-
-        @pl.when(col == 2)
-        def _():
-            send_both(k).wait_recv()
-            for j in (0, 1):
-                before[2 * k + j] = below[2 * k + j]
-
-        @pl.when(col == 3)
-        def _():
-            send_across(k).wait_recv()
-            send_both(k).wait_recv()
-            for j in (0, 1):
-                before[2 * k + j] = below[2 * k + j] + across[2 * k + j]
-
-        @pl.when(col < 3)
-        def _():
-            send_across(k).wait_send()
-
-        @pl.when(col < 2)
-        def _():
-            send_both(k).wait_send()
-
         wait_sent(1 - final, k)
         wait_passed(STEPS - 1, k)
-        done = field.at[final, pl.ds(2 + 2 * k, 2), cells, depth, :]
-        pltpu.make_async_copy(done, done, end_sem.at[k]).wait()
+        return 0
+
+    lax.fori_loop(0, CHUNKS, settle, 0)
+
+    def collect(k, _):
+        @pl.when(col > 0)
+        def _():
+            send_across(k, total).wait_recv()
         return 0
 
     lax.fori_loop(0, CHUNKS, collect, 0)
 
 
-def sums_kernel(end, before, column_sum, pressure_end):
-    so_far = before[0]
-    for x in range(CELLS):
-        here = end[0, x]
-        so_far = so_far + here
-        column_sum[0, x] = so_far * (1.0 / 32.0)
-        pressure_end[0, x] = here
+def sums_kernel(end, below, before, column_sum, pressure_end, sums, end_sem, sum_sem):
+    def copy(k, j):
+        y = (15 - k) if j else k
+        return pltpu.make_async_copy(end.at[2 * k + j], pressure_end.at[y], end_sem)
+
+    def store(k, j):
+        y = (15 - k) if j else k
+        return pltpu.make_async_copy(sums.at[2 * k + j], column_sum.at[y], sum_sem)
+
+    def one(k, _):
+        for j in (0, 1):
+            copy(k, j).start()
+            so_far = before[2 * k + j] + below[2 * k + j]
+            for x in range(CELLS):
+                so_far = so_far + end[2 * k + j, x]
+                sums[2 * k + j, x] = so_far * (1.0 / 32.0)
+            store(k, j).start()
+        return 0
+
+    lax.fori_loop(0, CHUNKS, one, 0)
+    pltpu.make_async_copy(end, pressure_end, end_sem).wait()
+    pltpu.make_async_copy(sums, column_sum, sum_sem).wait()
 
 
 def on_device(pressure, earlier, speed_square):
@@ -397,11 +412,12 @@
     f32 = jnp.float32
     block = (ROWS, CELLS, DEPTH, MEMBERS)
     plane = (ROWS, DEPTH, MEMBERS)
-    end, before = pl.pallas_call(
+    vmem = pl.BlockSpec(memory_space=pltpu.VMEM)
+    kept = pl.pallas_call(
         steps_kernel,
-        out_shape=(jax.ShapeDtypeStruct(block, f32), jax.ShapeDtypeStruct(plane, f32)),
+        out_shape=(pltpu.VMEM(block, f32), pltpu.VMEM(plane, f32), pltpu.VMEM(plane, f32)),
         in_specs=[whole] * 3,
-        out_specs=(whole, pl.BlockSpec(memory_space=pltpu.VMEM)),
+        out_specs=(vmem,) * 3,
         scratch_shapes=[
             pltpu.VMEM((2, ROWS + 2, CELLS + 2, DEPTH + 2 * PAD, MEMBERS), f32),
             pltpu.VMEM(block, f32),
@@ -410,37 +426,30 @@
             pltpu.VMEM((3, CHUNKS, DEPTH, MEMBERS), f32),
             pltpu.VMEM(plane, f32),
             pltpu.VMEM(plane, f32),
-            pltpu.VMEM(plane, f32),
-            pltpu.VMEM(plane, f32),
             dma((3, CHUNKS)),
             dma((2, 2, CHUNKS)), dma((2, 2, CHUNKS)),
             dma((2, 2)), dma((2, 2)),
             dma((2, 2, CHUNKS)), dma((2, 2, CHUNKS)),
             dma((3, CHUNKS)), dma((3, CHUNKS)),
-            dma((CHUNKS,)),
             dma((CHUNKS,)), dma((CHUNKS,)),
             dma((CHUNKS,)), dma((CHUNKS,)),
         ],
         compiler_params=pltpu.CompilerParams(
-            collective_id=0, has_side_effects=True, vmem_limit_bytes=56 * 1024 * 1024
+            collective_id=0, has_side_effects=True, vmem_limit_bytes=44 * 1024 * 1024
         ),
         name="steps",
     )(pressure, earlier, speed_square)
-
-    row = pl.BlockSpec((1, CELLS, DEPTH, MEMBERS), lambda y: (y, 0, 0, 0))
-
-    def place(y):
-        late = lax.div(y, ROWS // 2)
-        return ((1 - late) * 2 * y + late * (2 * (15 - y) + 1), 0, 0)
+    kept = [pltpu.with_memory_space_constraint(part, pltpu.VMEM) for part in kept]
 
     return pl.pallas_call(
         sums_kernel,
-        grid=(ROWS,),
         out_shape=(jax.ShapeDtypeStruct(block, f32), jax.ShapeDtypeStruct(block, f32)),
-        in_specs=[row, pl.BlockSpec((1, DEPTH, MEMBERS), place)],
-        out_specs=(row, row),
+        in_specs=[vmem] * 3,
+        out_specs=(whole, whole),
+        scratch_shapes=[pltpu.VMEM(block, f32), dma(()), dma(())],
+        compiler_params=pltpu.CompilerParams(vmem_limit_bytes=24 * 1024 * 1024),
         name="sums",
-    )(end, before)
+    )(*kept)
 
 
 def solution(mesh):

time: 294 us -> 274 us (0.932)
  Pallas kernels: 293 us -> 272 us
    pallas_call x2, Pallas kernels: 293 us -> 272 us  [the longest x1 266 us: on_device(): pl.pallas_call(steps_kernel, out_shape=(pltpu.VMEM(block, f32), pltpu.VME...]
where the time goes in v2:
time: 274 us; the launch traced here: 272 us
  Pallas kernels  272 us (99%)
    pallas_call x1, Pallas kernels, on_device(): pl.pallas_call(steps_kernel, out_shape=(pltpu.VMEM(block, f32), pltpu.VME...  266 us
    pallas_call x1, Pallas kernels, on_device(): pl.pallas_call(sums_kernel, out_shape=(jax.ShapeDtypeStruct(block, f32),...  5.81 us

profile of v2, /device:TPU:10, one launch (start us, length us, event | category | flops | bytes accessed | tf_op | source)
XLA Modules:
  0.0 272.5 jit_solution(14580893703189184876)
XLA Ops:
  0.6 266.0 %steps.1 = (f32[16,8,128,128]{3,2,1,0:T(8,128)S(1)}, f32[16,128,128]{2,1,0:T(8,128)S(1)}, f32[16,128,128]{2,1,0:T(8,128)S(1)}) custom-call(f32[16,8,128,128]{3,2,1,0:T(8,128)} %pressure.1, f32[16,8,128,128]{3,2,1,0:T(8,128)} %earlier.1, f32[16,8,128,128]{3,2,1,0:T(8,128)} %speed.1), custom_call_target="tpu_custom_call" | custom-call | tf_op jit(solution)/shard_map/steps/pallas_call | solution.py:416
  266.6 5.8 %sums.1 = (f32[16,8,128,128]{3,2,1,0:T(8,128)}, f32[16,8,128,128]{3,2,1,0:T(8,128)}) custom-call(f32[16,8,128,128]{3,2,1,0:T(8,128)S(1)} %get-tuple-element.5.end, f32[16,128,128]{2,1,0:T(8,128)S(1)} %get-tuple-element.6.below, f32[16,128,128]{2,1,0:T(8,128)S(1)} %get-tuple-element.7.before), custom_call_target="tpu_custom_call" | custom-call | tf_op jit(solution)/shard_map/sums/pallas_call | solution.py:444

commit v3 on v2

--- a/solution.py
+++ b/solution.py
@@ -15,6 +15,7 @@
 PIECE = 32
 LAG = 1
 LAG_UP = 1
+GROUP = 4
 
 
 def inner_place(k, j):
@@ -64,18 +65,24 @@
             dst = c.at[2 * k + j]
         else:
             dst = field.at[which, 2 + 2 * k + j, cells, depth, :]
-        return pltpu.make_async_copy(ref.at[y], dst, load_sem.at[which, k])
-
-    def wait_load(which, k):
-        if which == 2:
-            dst = c.at[pl.ds(2 * k, 2)]
-        else:
-            dst = field.at[which, pl.ds(2 + 2 * k, 2), cells, depth, :]
-        pltpu.make_async_copy(dst, dst, load_sem.at[which, k]).wait()
-
-    for which, ref in enumerate((pressure, earlier, speed)):
-        for j in (0, 1):
-            lax.fori_loop(0, CHUNKS, lambda k, _: (load(ref, which, k, j).start(), 0)[1], 0)
+        return pltpu.make_async_copy(ref.at[y], dst, (load_sem.at[3 + k] if which == 0 else load_sem.at[which]))
+
+    def wait_rows(k):
+        dst = field.at[0, pl.ds(2 + 2 * k, 2), cells, depth, :]
+        pltpu.make_async_copy(dst, dst, load_sem.at[3 + k]).wait()
+
+    def wait_load(which):
+        dst = c if which == 2 else field.at[which, pl.ds(2, ROWS), cells, depth, :]
+        pltpu.make_async_copy(dst, dst, load_sem.at[which]).wait()
+
+    def start_loads(which, ref):
+        def both_rows(k, _):
+            for j in (0, 1):
+                load(ref, which, k, j).start()
+            return 0
+        lax.fori_loop(0, CHUNKS, both_rows, 0)
+
+    start_loads(0, pressure)
 
     barrier = pltpu.get_barrier_semaphore()
     count = jnp.int32(1)
@@ -115,16 +122,20 @@
 
     pl.semaphore_wait(barrier, count)
 
+    def group(k):
+        g = lax.div(k, GROUP)
+        return g, pl.ds(2 * GROUP * g, 2 * GROUP)
+
     def x_pieces(slot, k, side):
         own, theirs = (CELLS, 0) if side else (1, CELLS + 1)
         places = pl.ds(2 + 2 * k, 2)
         return own, theirs, places
 
     def send_faces(t, k):
-        slot, third = lax.rem(t, 2), lax.rem(t, 3)
+        slot, fourth = lax.rem(t, 2), lax.rem(t, 4)
         for side in (1, 0):
             own, theirs, places = x_pieces(slot, k, side)
-            send, recv = send_x.at[side, slot, k], recv_x.at[1 - side, slot, k]
+            send, recv = send_x.at[side, slot], recv_x.at[1 - side, slot, k]
             middle = col == (1 if side else 2)
 
             @pl.when(has_col[side] & jnp.logical_not(middle))
@@ -137,8 +148,8 @@
             @pl.when(middle)
             def _():
                 remote(
-                    field.at[slot, 3 + 2 * k, own, depth, :], passing.at[third, k],
-                    send, pass_recv.at[third, k], other_y,
+                    field.at[slot, 3 + 2 * k, own, depth, :], passing.at[fourth, k],
+                    send, pass_recv.at[slot, k], other_y,
                 ).start()
                 remote(
                     field.at[slot, 2 + 2 * k, own, depth, :], field.at[slot, 2 + 2 * k, theirs, depth, :],
@@ -153,30 +164,30 @@
                     send_y.at[side, slot], recv_y.at[1 - side, slot], to_row[side],
                 ).start()
 
-            @pl.when(has_slab[side])
-            def _():
+            @pl.when(has_slab[side] & (lax.rem(k, GROUP) == GROUP - 1))
+            def _():
+                g, places = group(k)
                 remote(
-                    face.at[slot, side, pl.ds(2 * k, 2)], halo.at[slot, 1 - side, pl.ds(2 * k, 2)],
-                    send_z.at[side, slot, k], recv_z.at[1 - side, slot, k], to_slab[side],
+                    face.at[slot, side, places], halo.at[slot, 1 - side, places],
+                    send_z.at[side, slot], recv_z.at[1 - side, slot, g], to_slab[side],
                 ).start()
 
-    def wait_sent(slot, k):
+    def wait_sent(slot):
         for side in (0, 1):
             @pl.when(has_col[side])
             def _():
-                own, theirs, places = x_pieces(slot, k, side)
-                ref = field.at[slot, places, own, depth, :]
-                remote(ref, ref, send_x.at[side, slot, k], recv_x.at[side, slot, k], other_y).wait_send()
-
-            @pl.when(has_row[side] & (k == 0))
+                ref = field.at[slot, pl.ds(2, ROWS), CELLS if side else 1, depth, :]
+                remote(ref, ref, send_x.at[side, slot], recv_x.at[side, slot, 0], other_y).wait_send()
+
+            @pl.when(has_row[side])
             def _():
                 ref = field.at[slot, 2 + side, cells, depth, :]
                 remote(ref, ref, send_y.at[side, slot], recv_y.at[side, slot], other_y).wait_send()
 
             @pl.when(has_slab[side])
             def _():
-                ref = face.at[slot, side, pl.ds(2 * k, 2)]
-                remote(ref, ref, send_z.at[side, slot, k], recv_z.at[side, slot, k], other_y).wait_send()
+                ref = face.at[slot, side]
+                remote(ref, ref, send_z.at[side, slot], recv_z.at[side, slot, 0], other_y).wait_send()
 
     def wait_faces(slot, k):
         for side in (0, 1):
@@ -185,44 +196,42 @@
                 ref = field.at[slot, side, cells, depth, :]
                 remote(ref, ref, send_y.at[side, slot], recv_y.at[side, slot], other_y).wait_recv()
 
-            @pl.when(has_slab[side])
-            def _():
-                ref = halo.at[slot, side, pl.ds(2 * k, 2)]
-                remote(ref, ref, send_z.at[side, slot, k], recv_z.at[side, slot, k], other_y).wait_recv()
+            @pl.when(has_slab[side] & (lax.rem(k, GROUP) == 0))
+            def _():
+                g, places = group(k)
+                ref = halo.at[slot, side, places]
+                remote(ref, ref, send_z.at[side, slot], recv_z.at[side, slot, g], other_y).wait_recv()
 
         for side in (0, 1):
             @pl.when(has_col[side])
             def _():
                 ref = field.at[slot, pl.ds(2 + 2 * k, 2), side * (CELLS + 1), depth, :]
-                remote(ref, ref, send_x.at[side, slot, k], recv_x.at[side, slot, k], other_y).wait_recv()
-
-    def wait_passed(t, k):
+                remote(ref, ref, send_x.at[side, slot], recv_x.at[side, slot, k], other_y).wait_recv()
+
+    def wait_passed(t):
         @pl.when(relay)
         def _():
-            third = lax.rem(t, 3)
-            ref = passing.at[third, k]
-            remote(ref, ref, pass_send.at[third, k], pass_recv.at[third, k], other_y).wait_send()
+            ref = passing.at[lax.rem(t, 4)]
+            slot = lax.rem(t, 2)
+            remote(ref, ref, pass_send.at[slot], pass_recv.at[slot, 0], other_y).wait_send()
 
     def pass_on(message):
         t, k = lax.div(message, CHUNKS), lax.rem(message, CHUNKS)
-        slot, third = lax.rem(t, 2), lax.rem(t, 3)
-
-        @pl.when(t >= 1)
-        def _():
-            wait_passed(t - 1, k)
+        slot, fourth = lax.rem(t, 2), lax.rem(t, 4)
+
+        @pl.when((t >= 2) & (k == 0))
+        def _():
+            wait_passed(t - 2)
 
         @pl.when(relay)
         def _():
             side = 1 - at["y_lo"]
-            copy = remote(
-                passing.at[third, k], field.at[slot, 3 + 2 * k, side * (CELLS + 1), depth, :],
-                pass_send.at[third, k], recv_x.at[side, slot, k], other_x,
-            )
+            ref = passing.at[fourth, k]
+            remote(ref, ref, pass_send.at[slot], pass_recv.at[slot, k], other_y).wait_recv()
             remote(
-                passing.at[third, k], passing.at[third, k],
-                pass_send.at[third, k], pass_recv.at[third, k], other_y,
-            ).wait_recv()
-            copy.start()
+                ref, field.at[slot, 3 + 2 * k, side * (CELLS + 1), depth, :],
+                pass_send.at[slot], recv_x.at[side, slot, k], other_x,
+            ).start()
 
     def advance(slot, k, last):
         for j in (0, 1):
@@ -267,7 +276,7 @@
                 face[slot, 1, 2 * k + j, x:x + 1, :] = field[slot, place, 1 + x, PAD + DEPTH - 1:PAD + DEPTH, :]
 
     def start(k, _):
-        wait_load(0, k)
+        wait_rows(k)
         take_ends(0, k)
         send_faces(jnp.int32(0), k)
 
@@ -277,21 +286,23 @@
         return 0
 
     lax.fori_loop(0, CHUNKS, start, 0)
+    start_loads(1, earlier)
+    start_loads(2, speed)
 
     def main(n, _):
         t, k = lax.div(n, CHUNKS), lax.rem(n, CHUNKS)
         slot = lax.rem(t, 2)
 
-        @pl.when(n < CHUNKS)
-        def _():
-            wait_load(1, k)
-            wait_load(2, k)
-
         wait_faces(slot, k)
 
-        @pl.when(n >= CHUNKS)
-        def _():
-            wait_sent(1 - slot, k)
+        @pl.when(n == 0)
+        def _():
+            wait_load(1)
+            wait_load(2)
+
+        @pl.when((t >= 1) & (k == 0))
+        def _():
+            wait_sent(1 - slot)
 
         advance(slot, k, False)
         take_ends(1 - slot, k)
@@ -310,10 +321,10 @@
         return pl.ds(2 * k, 2)
 
     def send_up(k):
-        return remote(total.at[chunk(k)], below.at[chunk(k)], up_send.at[k], up_recv.at[k], other_y)
+        return remote(total.at[chunk(k)], below.at[chunk(k)], up_send.at[0], up_recv.at[k], other_y)
 
     def send_across(k, source):
-        return remote(source.at[chunk(k)], before.at[chunk(k)], across_send.at[k], across_recv.at[k], other_x)
+        return remote(source.at[chunk(k)], before.at[chunk(k)], across_send.at[0], across_recv.at[0], other_x)
 
     def from_below(k):
         @pl.when(jnp.logical_not(early))
@@ -351,35 +362,28 @@
     for k in range(CHUNKS - LAG_UP, CHUNKS):
         from_below(k)
 
-    def settle(k, _):
-        @pl.when(col == 0)
-        def _():
-            for j in (0, 1):
-                before[2 * k + j] = zeros
-
-        @pl.when(early)
-        def _():
-            for j in (0, 1):
-                below[2 * k + j] = zeros
-            send_up(k).wait_send()
-
-        @pl.when(col != 1)
-        def _():
-            send_across(k, total).wait_send()
-        wait_sent(final, k)
-        wait_sent(1 - final, k)
-        wait_passed(STEPS - 1, k)
-        return 0
-
-    lax.fori_loop(0, CHUNKS, settle, 0)
-
-    def collect(k, _):
-        @pl.when(col > 0)
-        def _():
-            send_across(k, total).wait_recv()
-        return 0
-
-    lax.fori_loop(0, CHUNKS, collect, 0)
+    everything = remote(total, before, across_send.at[0], across_recv.at[0], other_x)
+
+    @pl.when(early)
+    def _():
+        below[...] = jnp.zeros_like(below)
+        remote(total, below, up_send.at[0], up_recv.at[0], other_y).wait_send()
+
+    @pl.when(col == 0)
+    def _():
+        before[...] = jnp.zeros_like(before)
+
+    for t in (STEPS - 2, STEPS - 1):
+        wait_sent(jnp.int32(t % 2))
+        wait_passed(jnp.int32(t))
+
+    @pl.when(col != 1)
+    def _():
+        everything.wait_send()
+
+    @pl.when(col > 0)
+    def _():
+        everything.wait_recv()
 
 
 def sums_kernel(end, below, before, column_sum, pressure_end, sums, end_sem, sum_sem):
@@ -423,16 +427,16 @@
             pltpu.VMEM(block, f32),
             pltpu.VMEM((2, 2, ROWS, CELLS, MEMBERS), f32),
             pltpu.VMEM((2, 2, ROWS, CELLS, MEMBERS), f32),
-            pltpu.VMEM((3, CHUNKS, DEPTH, MEMBERS), f32),
+            pltpu.VMEM((4, CHUNKS, DEPTH, MEMBERS), f32),
             pltpu.VMEM(plane, f32),
             pltpu.VMEM(plane, f32),
-            dma((3, CHUNKS)),
-            dma((2, 2, CHUNKS)), dma((2, 2, CHUNKS)),
+            dma((3 + CHUNKS,)),
+            dma((2, 2)), dma((2, 2, CHUNKS)),
             dma((2, 2)), dma((2, 2)),
-            dma((2, 2, CHUNKS)), dma((2, 2, CHUNKS)),
-            dma((3, CHUNKS)), dma((3, CHUNKS)),
-            dma((CHUNKS,)), dma((CHUNKS,)),
-            dma((CHUNKS,)), dma((CHUNKS,)),
+            dma((2, 2)), dma((2, 2, CHUNKS // GROUP)),
+            dma((2,)), dma((2, CHUNKS)),
+            dma((1,)), dma((CHUNKS,)),
+            dma((1,)), dma((1,)),
         ],
         compiler_params=pltpu.CompilerParams(
             collective_id=0, has_side_effects=True, vmem_limit_bytes=44 * 1024 * 1024

time: 274 us -> 272 us (level)
  no operation moved by 1% of the time
where the time goes in v3:
time: 272 us; the launch traced here: 271 us
  Pallas kernels  270 us (99%)
    pallas_call x1, Pallas kernels, on_device(): pl.pallas_call(steps_kernel, out_shape=(pltpu.VMEM(block, f32), pltpu.VME...  264 us
    pallas_call x1, Pallas kernels, on_device(): pl.pallas_call(sums_kernel, out_shape=(jax.ShapeDtypeStruct(block, f32),...  5.81 us

profile of v3, /device:TPU:10, one launch (start us, length us, event | category | flops | bytes accessed | tf_op | source)
XLA Modules:
  0.0 270.8 jit_solution(9813381632399493704)
XLA Ops:
  0.6 264.4 %steps.1 = (f32[16,8,128,128]{3,2,1,0:T(8,128)S(1)}, f32[16,128,128]{2,1,0:T(8,128)S(1)}, f32[16,128,128]{2,1,0:T(8,128)S(1)}) custom-call(f32[16,8,128,128]{3,2,1,0:T(8,128)} %pressure.1, f32[16,8,128,128]{3,2,1,0:T(8,128)} %earlier.1, f32[16,8,128,128]{3,2,1,0:T(8,128)} %speed.1), custom_call_target="tpu_custom_call" | custom-call | tf_op jit(solution)/shard_map/steps/pallas_call | solution.py:420
  265.0 5.8 %sums.1 = (f32[16,8,128,128]{3,2,1,0:T(8,128)}, f32[16,8,128,128]{3,2,1,0:T(8,128)}) custom-call(f32[16,8,128,128]{3,2,1,0:T(8,128)S(1)} %get-tuple-element.5.end, f32[16,128,128]{2,1,0:T(8,128)S(1)} %get-tuple-element.6.below, f32[16,128,128]{2,1,0:T(8,128)S(1)} %get-tuple-element.7.before), custom_call_target="tpu_custom_call" | custom-call | tf_op jit(solution)/shard_map/sums/pallas_call | solution.py:448

commit v4 on v3

--- a/solution.py
+++ b/solution.py
@@ -14,8 +14,8 @@
 PAD = 8
 PIECE = 32
 LAG = 1
-LAG_UP = 1
 GROUP = 4
+FIRST, LAST = 4, 6
 
 
 def inner_place(k, j):
@@ -39,7 +39,7 @@
     pressure, earlier, speed, end, below, before,
     field, c, face, halo, passing, total, both,
     load_sem, send_x, recv_x, send_y, recv_y, send_z, recv_z, pass_send, pass_recv,
-    up_send, up_recv, across_send, across_recv,
+    up_send, up_recv, across_send, across_recv, detour, detour_send, detour_recv,
 ):
     at, row, col, slab = where_am_i()
     col_lo, col_hi = step_to(col, -1, ("y_lo", "x_hi")), step_to(col, 1, ("y_lo", "x_hi"))
@@ -52,6 +52,8 @@
     has_slab = (slab > 0, slab < 7)
     to_col, to_row, to_slab = (col_lo, col_hi), (row_lo, row_hi), (slab_lo, slab_hi)
     relay = (col == 0) | (col == 3)
+    other_row = {"x_lo": 1 - at["x_lo"]}
+    other_both = {"x_lo": 1 - at["x_lo"], "x_hi": 1 - at["x_hi"]}
     cells, depth = pl.ds(1, CELLS), pl.ds(PAD, DEPTH)
 
     def remote(src, dst, send, recv, device):
@@ -85,14 +87,15 @@
     start_loads(0, pressure)
 
     barrier = pltpu.get_barrier_semaphore()
-    count = jnp.int32(1)
+    count = jnp.int32(3)
     for has, to in ((has_col, to_col), (has_row, to_row), (has_slab, to_slab)):
         for side in (0, 1):
             @pl.when(has[side])
             def _():
                 pl.semaphore_signal(barrier, inc=1, device_id=to[side], device_id_type=MESH)
             count = count + has[side].astype(jnp.int32)
-    pl.semaphore_signal(barrier, inc=1, device_id=other_y, device_id_type=MESH)
+    for other in (other_y, other_row, other_both):
+        pl.semaphore_signal(barrier, inc=1, device_id=other, device_id_type=MESH)
 
     zeros = jnp.zeros((DEPTH, MEMBERS), jnp.float32)
     for side in (0, 1):
@@ -157,7 +160,7 @@
                 ).start()
 
         for side in (0, 1):
-            @pl.when(has_row[side] & (k == 0))
+            @pl.when(has_row[side] & (k == lax.div(t, STEPS - 1) * (CHUNKS - 1)))
             def _():
                 remote(
                     field.at[slot, 2 + side, cells, depth, :], field.at[slot, 1 - side, cells, depth, :],
@@ -189,14 +192,14 @@
                 ref = face.at[slot, side]
                 remote(ref, ref, send_z.at[side, slot], recv_z.at[side, slot, 0], other_y).wait_send()
 
-    def wait_faces(slot, k):
+    def wait_faces(slot, k, opens_group):
         for side in (0, 1):
             @pl.when(has_row[side] & (k == 0))
             def _():
                 ref = field.at[slot, side, cells, depth, :]
                 remote(ref, ref, send_y.at[side, slot], recv_y.at[side, slot], other_y).wait_recv()
 
-            @pl.when(has_slab[side] & (lax.rem(k, GROUP) == 0))
+            @pl.when(has_slab[side] & opens_group)
             def _():
                 g, places = group(k)
                 ref = halo.at[slot, side, places]
@@ -293,7 +296,7 @@
         t, k = lax.div(n, CHUNKS), lax.rem(n, CHUNKS)
         slot = lax.rem(t, 2)
 
-        wait_faces(slot, k)
+        wait_faces(slot, k, lax.rem(k, GROUP) == 0)
 
         @pl.when(n == 0)
         def _():
@@ -316,6 +319,8 @@
 
     final = STEPS % 2
     early = at["y_lo"] == 0
+    late = at["x_hi"] == 1
+    heavy = (row == 1) | (row == 2)
 
     def chunk(k):
         return pl.ds(2 * k, 2)
@@ -324,7 +329,21 @@
         return remote(total.at[chunk(k)], below.at[chunk(k)], up_send.at[0], up_recv.at[k], other_y)
 
     def send_across(k, source):
-        return remote(source.at[chunk(k)], before.at[chunk(k)], across_send.at[0], across_recv.at[0], other_x)
+        @pl.when(jnp.logical_not(heavy & (k >= FIRST) & (k < LAST)))
+        def _():
+            remote(
+                source.at[chunk(k)], before.at[chunk(k)], across_send.at[0], across_recv.at[0], other_x
+            ).start()
+
+        @pl.when(heavy & (k >= FIRST) & (k < LAST))
+        def _():
+            remote(
+                source.at[chunk(k)], detour.at[chunk(k - FIRST)],
+                across_send.at[0], detour_recv.at[k - FIRST], other_both,
+            ).start()
+
+    def send_half(place, source, device):
+        remote(source.at[place], before.at[place], across_send.at[0], across_recv.at[0], device).start()
 
     def from_below(k):
         @pl.when(jnp.logical_not(early))
@@ -335,14 +354,19 @@
         def _():
             for j in (0, 1):
                 both[2 * k + j] = total[2 * k + j] + below[2 * k + j]
-            send_across(k, both).start()
+            send_across(k, both)
 
         @pl.when(col == 3)
         def _():
-            send_across(k, below).start()
-
-    def finish(k, _):
-        wait_faces(1 - final, k)
+            send_half(2 * k + 1, below, other_x)
+
+    def finish(i, _):
+        k = lax.rem(i + 1, CHUNKS)
+
+        @pl.when(i >= 1)
+        def _():
+            from_below(i)
+        wait_faces(1 - final, k, (k == 1) | (k == GROUP))
         advance(1 - final, k, True)
 
         @pl.when(early)
@@ -351,16 +375,24 @@
 
         @pl.when(col == 0)
         def _():
-            send_across(k, total).start()
-
-        @pl.when(k >= LAG_UP)
-        def _():
-            from_below(k - LAG_UP)
+            send_across(k, total)
+
+        @pl.when(col == 1)
+        def _():
+            send_half(2 * k, total, col_hi)
         return 0
 
     lax.fori_loop(0, CHUNKS, finish, 0)
-    for k in range(CHUNKS - LAG_UP, CHUNKS):
-        from_below(k)
+    from_below(jnp.int32(0))
+
+    @pl.when(late & jnp.logical_not(heavy))
+    def _():
+        for d in range(LAST - FIRST):
+            ref = detour.at[chunk(d)]
+            remote(ref, ref, detour_send.at[0], detour_recv.at[d], other_both).wait_recv()
+            remote(
+                ref, before.at[chunk(FIRST + d)], detour_send.at[0], across_recv.at[0], other_row
+            ).start()
 
     everything = remote(total, before, across_send.at[0], across_recv.at[0], other_x)
 
@@ -377,9 +409,18 @@
         wait_sent(jnp.int32(t % 2))
         wait_passed(jnp.int32(t))
 
-    @pl.when(col != 1)
+    @pl.when(jnp.logical_not(late))
     def _():
         everything.wait_send()
+
+    @pl.when(late)
+    def _():
+        half = total.at[pl.ds(0, ROWS // 2)]
+        remote(half, half, across_send.at[0], across_recv.at[0], other_x).wait_send()
+
+    @pl.when(late & jnp.logical_not(heavy))
+    def _():
+        remote(detour, detour, detour_send.at[0], detour_recv.at[0], other_row).wait_send()
 
     @pl.when(col > 0)
     def _():
@@ -437,6 +478,7 @@
             dma((2,)), dma((2, CHUNKS)),
             dma((1,)), dma((CHUNKS,)),
             dma((1,)), dma((1,)),
+            pltpu.VMEM((2 * (LAST - FIRST), DEPTH, MEMBERS), f32), dma((1,)), dma((LAST - FIRST,)),
         ],
         compiler_params=pltpu.CompilerParams(
             collective_id=0, has_side_effects=True, vmem_limit_bytes=44 * 1024 * 1024

time: 272 us -> 270 us (level)
  no operation moved by 1% of the time
where the time goes in v4:
time: 270 us
  Pallas kernels  270 us (100%)
    pallas_call x1, Pallas kernels, on_device(): pl.pallas_call(steps_kernel, out_shape=(pltpu.VMEM(block, f32), pltpu.VME...  264 us
    pallas_call x1, Pallas kernels, on_device(): pl.pallas_call(sums_kernel, out_shape=(jax.ShapeDtypeStruct(block, f32),...  5.81 us

profile of v4, /device:TPU:10, one launch (start us, length us, event | category | flops | bytes accessed | tf_op | source)
XLA Modules:
  0.0 270.4 jit_solution(5808473292519138389)
XLA Ops:
  0.6 263.9 %steps.1 = (f32[16,8,128,128]{3,2,1,0:T(8,128)S(1)}, f32[16,128,128]{2,1,0:T(8,128)S(1)}, f32[16,128,128]{2,1,0:T(8,128)S(1)}) custom-call(f32[16,8,128,128]{3,2,1,0:T(8,128)} %pressure.1, f32[16,8,128,128]{3,2,1,0:T(8,128)} %earlier.1, f32[16,8,128,128]{3,2,1,0:T(8,128)} %speed.1), custom_call_target="tpu_custom_call" | custom-call | tf_op jit(solution)/shard_map/steps/pallas_call | solution.py:461
  264.5 5.8 %sums.1 = (f32[16,8,128,128]{3,2,1,0:T(8,128)}, f32[16,8,128,128]{3,2,1,0:T(8,128)}) custom-call(f32[16,8,128,128]{3,2,1,0:T(8,128)S(1)} %get-tuple-element.5.end, f32[16,128,128]{2,1,0:T(8,128)S(1)} %get-tuple-element.6.below, f32[16,128,128]{2,1,0:T(8,128)S(1)} %get-tuple-element.7.before), custom_call_target="tpu_custom_call" | custom-call | tf_op jit(solution)/shard_map/sums/pallas_call | solution.py:490

commit v5 on v4

--- a/solution.py
+++ b/solution.py
@@ -358,7 +358,9 @@
 
         @pl.when(col == 3)
         def _():
-            send_half(2 * k + 1, below, other_x)
+            @pl.when(k > 0)
+            def _():
+                send_half(2 * k + 1, below, other_x)
 
     def finish(i, _):
         k = lax.rem(i + 1, CHUNKS)
@@ -380,6 +382,10 @@
         @pl.when(col == 1)
         def _():
             send_half(2 * k, total, col_hi)
+
+            @pl.when(k == 0)
+            def _():
+                send_half(1, total, col_hi)
         return 0
 
     lax.fori_loop(0, CHUNKS, finish, 0)
@@ -415,8 +421,11 @@
 
     @pl.when(late)
     def _():
-        half = total.at[pl.ds(0, ROWS // 2)]
-        remote(half, half, across_send.at[0], across_recv.at[0], other_x).wait_send()
+        for block, count_of in ((1, ROWS // 2 + 1), (3, ROWS // 2 - 1)):
+            @pl.when(col == block)
+            def _():
+                part = total.at[pl.ds(0, count_of)]
+                remote(part, part, across_send.at[0], across_recv.at[0], other_x).wait_send()
 
     @pl.when(late & jnp.logical_not(heavy))
     def _():

time: 270 us -> 269 us (level)
  no operation moved by 1% of the time
where the time goes in v5:
time: 269 us
  Pallas kernels  268 us (100%)
    pallas_call x1, Pallas kernels, on_device(): pl.pallas_call(steps_kernel, out_shape=(pltpu.VMEM(block, f32), pltpu.VME...  263 us
    pallas_call x1, Pallas kernels, on_device(): pl.pallas_call(sums_kernel, out_shape=(jax.ShapeDtypeStruct(block, f32),...  5.81 us

profile of v5, /device:TPU:10, one launch (start us, length us, event | category | flops | bytes accessed | tf_op | source)
XLA Modules:
  0.0 269.0 jit_solution(1532271859679378135)
XLA Ops:
  0.6 262.5 %steps.1 = (f32[16,8,128,128]{3,2,1,0:T(8,128)S(1)}, f32[16,128,128]{2,1,0:T(8,128)S(1)}, f32[16,128,128]{2,1,0:T(8,128)S(1)}) custom-call(f32[16,8,128,128]{3,2,1,0:T(8,128)} %pressure.1, f32[16,8,128,128]{3,2,1,0:T(8,128)} %earlier.1, f32[16,8,128,128]{3,2,1,0:T(8,128)} %speed.1), custom_call_target="tpu_custom_call" | custom-call | tf_op jit(solution)/shard_map/steps/pallas_call | solution.py:470
  263.1 5.8 %sums.1 = (f32[16,8,128,128]{3,2,1,0:T(8,128)}, f32[16,8,128,128]{3,2,1,0:T(8,128)}) custom-call(f32[16,8,128,128]{3,2,1,0:T(8,128)S(1)} %get-tuple-element.5.end, f32[16,128,128]{2,1,0:T(8,128)S(1)} %get-tuple-element.6.below, f32[16,128,128]{2,1,0:T(8,128)S(1)} %get-tuple-element.7.before), custom_call_target="tpu_custom_call" | custom-call | tf_op jit(solution)/shard_map/sums/pallas_call | solution.py:499

commit v6 on v5

--- a/solution.py
+++ b/solution.py
@@ -134,7 +134,7 @@
         places = pl.ds(2 + 2 * k, 2)
         return own, theirs, places
 
-    def send_faces(t, k):
+    def send_faces(t, k, ends_after=False):
         slot, fourth = lax.rem(t, 2), lax.rem(t, 4)
         for side in (1, 0):
             own, theirs, places = x_pieces(slot, k, side)
@@ -159,6 +159,8 @@
                     send, recv, to_col[side],
                 ).start()
 
+        if ends_after:
+            take_ends(slot, k)
         for side in (0, 1):
             @pl.when(has_row[side] & (k == lax.div(t, STEPS - 1) * (CHUNKS - 1)))
             def _():
@@ -280,8 +282,7 @@
 
     def start(k, _):
         wait_rows(k)
-        take_ends(0, k)
-        send_faces(jnp.int32(0), k)
+        send_faces(jnp.int32(0), k, ends_after=True)
 
         @pl.when(k >= LAG)
         def _():

time: 269 us -> 269 us (level)
  no operation moved by 1% of the time
where the time goes in v6:
time: 269 us
  Pallas kernels  268 us (100%)
    pallas_call x1, Pallas kernels, on_device(): pl.pallas_call(steps_kernel, out_shape=(pltpu.VMEM(block, f32), pltpu.VME...  262 us
    pallas_call x1, Pallas kernels, on_device(): pl.pallas_call(sums_kernel, out_shape=(jax.ShapeDtypeStruct(block, f32),...  5.81 us

profile of v6, /device:TPU:10, one launch (start us, length us, event | category | flops | bytes accessed | tf_op | source)
XLA Modules:
  0.0 268.9 jit_solution(1712983072848413667)
XLA Ops:
  0.6 262.5 %steps.1 = (f32[16,8,128,128]{3,2,1,0:T(8,128)S(1)}, f32[16,128,128]{2,1,0:T(8,128)S(1)}, f32[16,128,128]{2,1,0:T(8,128)S(1)}) custom-call(f32[16,8,128,128]{3,2,1,0:T(8,128)} %pressure.1, f32[16,8,128,128]{3,2,1,0:T(8,128)} %earlier.1, f32[16,8,128,128]{3,2,1,0:T(8,128)} %speed.1), custom_call_target="tpu_custom_call" | custom-call | tf_op jit(solution)/shard_map/steps/pallas_call | solution.py:471
  263.1 5.8 %sums.1 = (f32[16,8,128,128]{3,2,1,0:T(8,128)}, f32[16,8,128,128]{3,2,1,0:T(8,128)}) custom-call(f32[16,8,128,128]{3,2,1,0:T(8,128)S(1)} %get-tuple-element.5.end, f32[16,128,128]{2,1,0:T(8,128)S(1)} %get-tuple-element.6.below, f32[16,128,128]{2,1,0:T(8,128)S(1)} %get-tuple-element.7.before), custom_call_target="tpu_custom_call" | custom-call | tf_op jit(solution)/shard_map/sums/pallas_call | solution.py:500
